TPU v7x, 64 devices: a 2x2x8 block of a 4x4x8 slice. The times are simulated.
64 devices in a mesh: dp: 4 (over x, y), ep: 16 (over z, core).
Axes of the slice: x: 2, y: 2, z: 8, core: 2. Of those that a mesh axis runs over, the one named last changes fastest.
The devices are a block of a 4x4x8 slice.
Arguments:
- x_rows: bfloat16 [32768, 768], P(('dp', 'ep')), parts along dimension 0
- logits: float32 [32768, 64], P(('dp', 'ep')), parts along dimension 0
- w_in: bfloat16 [64, 768, 3072], P('ep')
- w_out: bfloat16 [64, 3072, 768], P('ep')
Outputs:
- output: bfloat16 [32768, 768], P(('dp', 'ep')), parts along dimension 0
There are 4 independent parts. A program takes and returns all parts, laid end to end along the dimension named above; an argument that names none is the same for every part.
All inputs are finite; a program needn't handle non-finite values.
Results may differ from a plain program's by a relative error of at most 0.001.
Values are sent between devices in bfloat16 or wider.
A program may use at most 768 MiB of HBM per device.

v0:
```python
import jax
import jax.numpy as jnp
from jax import lax
from jax.sharding import PartitionSpec as P

CAP_FACTOR = 2


def solution(mesh):
    group_size = mesh.shape['ep']
    row_spec = P(('dp', 'ep'), None)
    expert_spec = P('ep', None, None)

    def local_step(x_rows, logits, w_in, w_out):
        tok_dev, d_model = x_rows.shape
        experts = logits.shape[1]
        exp_dev = w_in.shape[0]
        capacity = CAP_FACTOR * tok_dev * group_size // experts
        src_cap = 4 * tok_dev // experts
        my_index = lax.axis_index('ep')
        gate_probs = jax.nn.softmax(logits, axis=-1)
        top_vals, top_ids = lax.top_k(logits, 2)
        chosen = (logits >= top_vals[:, 1:2]).astype(jnp.int32)
        local_before = jnp.cumsum(chosen, axis=0) - chosen
        local_counts = jnp.sum(chosen, axis=0).astype(jnp.float32)
        all_counts = lax.all_gather(local_counts, 'ep').astype(jnp.int32)
        dev_offsets = jnp.cumsum(all_counts, axis=0) - all_counts
        local_pos = jnp.take_along_axis(local_before, top_ids, axis=1)
        kept_mask = local_pos + jnp.take(dev_offsets[my_index], top_ids) < capacity
        send_row = jnp.where(kept_mask, top_ids * src_cap + local_pos, experts * src_cap)
        tok_ids = jnp.broadcast_to(jnp.arange(tok_dev, dtype=jnp.int32)[:, None], (tok_dev, 2))
        slot_tok = jnp.full((experts * src_cap,), tok_dev, jnp.int32).at[send_row.reshape(-1)].set(tok_ids.reshape(-1), mode='drop')
        send_buf = jnp.take(x_rows, slot_tok, axis=0, mode='fill', fill_value=0)
        recv_buf = lax.all_to_all(send_buf, 'ep', 0, 0, tiled=True)

        own_counts = lax.dynamic_slice_in_dim(all_counts, my_index * exp_dev, exp_dev, axis=1)
        own_offsets = lax.dynamic_slice_in_dim(dev_offsets, my_index * exp_dev, exp_dev, axis=1)
        kept_counts = jnp.minimum(jnp.maximum(capacity - own_offsets, 0), own_counts)
        slot_ends = (own_offsets + kept_counts).T
        cap_ids = jnp.arange(capacity, dtype=jnp.int32)
        below_mask = slot_ends[:, None, :] <= cap_ids[None, :, None]
        src_dev = jnp.sum(below_mask.astype(jnp.int32), axis=2)
        slot_start = jnp.sum(jnp.where(below_mask, kept_counts.T[:, None, :], 0), axis=2)
        exp_local = jnp.arange(exp_dev, dtype=jnp.int32)
        recv_row = (src_dev * exp_dev + exp_local[:, None]) * src_cap + cap_ids[None, :] - slot_start
        recv_row = jnp.where(src_dev < group_size, recv_row, group_size * exp_dev * src_cap)
        expert_rows = jnp.take(recv_buf, recv_row.reshape(-1), axis=0, mode='fill', fill_value=0).reshape(exp_dev, capacity, d_model)
        hidden = jax.nn.gelu(jnp.einsum('ecd,edf->ecf', expert_rows, w_in, preferred_element_type=jnp.float32), approximate=True).astype(jnp.bfloat16)
        expert_out = jnp.einsum('ecf,efd->ecd', hidden, w_out, preferred_element_type=jnp.float32).astype(jnp.bfloat16).reshape(exp_dev * capacity, d_model)

        src_slots = jnp.arange(src_cap, dtype=jnp.int32)
        back_row = exp_local[None, :, None] * capacity + own_offsets[:, :, None] + src_slots[None, None, :]
        back_row = jnp.where(src_slots[None, None, :] < kept_counts[:, :, None], back_row, exp_dev * capacity)
        back_buf = jnp.take(expert_out, back_row.reshape(-1), axis=0, mode='fill', fill_value=0)
        ret_buf = lax.all_to_all(back_buf, 'ep', 0, 0, tiled=True)

        rows_back = jnp.take(ret_buf, send_row, axis=0, mode='fill', fill_value=0)
        pick_gate = jnp.take_along_axis(gate_probs, top_ids, axis=1)
        mix_sum = jnp.sum(pick_gate[:, :, None] * rows_back.astype(jnp.float32), axis=1)
        return (x_rows.astype(jnp.float32) + mix_sum).astype(jnp.bfloat16)

    return jax.shard_map(local_step, mesh=mesh, in_specs=(row_spec, row_spec, expert_spec, expert_spec), out_specs=row_spec, check_vma=False)
```

profile of v0, /device:TPU:21, one launch (start us, length us, event | category | flops | bytes accessed | tf_op | source)
XLA Modules:
  0.0 318.4 jit_solution(790478958459595974)
XLA Ops:
  0.0 2.8 top_k.11
  2.8 1.1 convert_reduce_fusion
  3.9 1.3 dynamic-slice
  6.1 28.8 %all-reduce = f32[1024]{0:T(1024)S(1)} all-reduce(f32[1024]{0:T(1024)S(1)} %convert_dynamic-update-slice_fusion), channel_id=2, replica_groups=mesh['dp'=4,'ep'=16] {'ep'}, use_global_device_ids=true, to_apply=%add | all-reduce | flops 1024 | bytes 8192
  35.0 0.7 fusion.43
  37.9 1.2 reduce-window.6
  39.8 8.6 %gather_fusion.5 = s32[1024]{0:T(1024)S(1)} fusion(s32[512,64]{0,1:T(8,128)S(1)} %convert_subtract_fusion, s32[1024]{0:T(1024)S(1)} %reshape.389), kind=kCustom, calls=%fused_computation.5 | custom fusion | bytes 16384 | tf_op jit(solution)/shard_map/jit(take_along_axis)/gather | solution.py:28
  48.8 40.0 %compare_and_fusion.1 = (pred[512,2]{0,1:T(4,128)(4,1)S(1)}, s32[512,2]{0,1:T(2,128)S(1)}) fusion(s32[]{:T(128)} %bitcast.68, s32[]{:T(128)} %bitcast.67, s32[]{:T(128)} %bitcast.66, s32[]{:T(128)} %bitcast.65, s32[]{:T(128)} %bitcast.64, s32[]{:T(128)} %bitcast.63, s32[]{:T(128)} %bitcast.62, s32[]{:T(128)} %bitcast.61, s32[]{:T(128)} %bitcast.60, ...), kind=kLoop, calls=%fused_computation.122 | loop fusion | flops 148480 | bytes 13568 | tf_op jit(solution)/shard_map/jit(_take)/and | solution.py:57
  89.4 4.3 %scatter_custom_fusion = s32[2048]{0:T(1024)S(1)} fusion(s32[1024]{0:T(1024)S(1)} %bitcast.117, s32[1024]{0:T(1024)S(1)} %reshape.405, s32[]{:T(128)} %constant.106.clone.1), kind=kCustom, calls=%fused_computation.131 | custom fusion | bytes 8196 | tf_op jit(solution)/shard_map/scatter | solution.py:32
  93.7 9.4 %gather_fusion = bf16[2048,768]{1,0:T(8,128)(2,1)} fusion(bf16[512,768]{1,0:T(8,128)(2,1)S(1)} %copy-done, s32[2048]{0:T(1024)S(1)} %fusion.29), kind=kCustom, calls=%fused_computation | custom fusion | bytes 6299648 | tf_op jit(solution)/shard_map/jit(_take)/gather | solution.py:33
  103.1 3.3 %broadcast_select_fusion = bf16[16,128,768]{2,1,0:T(8,128)(2,1)} fusion(bf16[16,128,768]{2,1,0:T(8,128)(2,1)} %bitcast.110, pred[16,128]{1,0:T(8,128)(4,1)S(1)} %and_bitcast_fusion), kind=kLoop, calls=%fused_computation.22 | loop fusion | flops 1572864 | bytes 6293504 | tf_op jit(solution)/shard_map/jit(_take)/select_n | solution.py:33
  106.4 7.2 %all-to-all-start = ((bf16[16,128,768]{2,1,0:T(8,128)(2,1)}), bf16[16,128,768]{2,1,0:T(8,128)(2,1)}, u32[]{:S(2)}, u32[]{:S(2)}) async-start(bf16[16,128,768]{2,1,0:T(8,128)(2,1)} %broadcast_select_fusion), calls=%async_computation | async-start | bytes 6291456 | tf_op jit(solution)/shard_map/all_to_all | solution.py:34
  114.4 70.6 %all-to-all-done = bf16[16,128,768]{2,1,0:T(8,128)(2,1)} async-done(((bf16[16,128,768]{2,1,0:T(8,128)(2,1)}), bf16[16,128,768]{2,1,0:T(8,128)(2,1)}, u32[]{:S(2)}, u32[]{:S(2)}) %all-to-all-start) | async-done | bytes 3145760 | tf_op jit(solution)/shard_map/all_to_all | solution.py:34
  185.0 6.8 %gather_fusion.1 = bf16[1024,768]{1,0:T(8,128)(2,1)S(1)} fusion(bf16[2048,768]{1,0:T(8,128)(2,1)} %bitcast.74, s32[1024]{0:T(1024)S(1)} %broadcast_clamp_fusion.2), kind=kCustom, calls=%fused_computation.1 | custom fusion | bytes 3149824 | tf_op jit(solution)/shard_map/jit(_take)/gather | solution.py:47
  191.7 17.2 %fusion.14 = bf16[4,256,768]{2,1,0:T(8,128)(2,1)S(1)} fusion(bf16[4,3072,768]{2,1,0:T(8,128)(2,1)} %param.7, bf16[4,768,3072]{2,1,0:T(8,128)(2,1)} %param.6, bf16[4,256,768]{2,1,0:T(8,128)(2,1)S(1)} %bitcast.111, pred[4,256]{1,0:T(4,128)(4,1)S(1)} %compare_and_fusion.3), kind=kOutput, calls=%fused_computation.25 | convolution fusion | flops 9693560832 | bytes 40895488 | tf_op jit(solution)/shard_map/ecf,efd->ecd/dot_general | solution.py:49
  209.0 9.4 %gather_fusion.2 = bf16[2048,768]{1,0:T(8,128)(2,1)} fusion(bf16[1024,768]{1,0:T(8,128)(2,1)S(1)} %bitcast.108, s32[2048]{0:T(1024)S(1)} %broadcast_clamp_fusion), kind=kCustom, calls=%fused_computation.2 | custom fusion | bytes 6299648 | tf_op jit(solution)/shard_map/jit(_take)/gather | solution.py:54
  218.3 3.3 %broadcast_select_fusion.1 = bf16[16,128,768]{2,1,0:T(8,128)(2,1)} fusion(bf16[16,128,768]{2,1,0:T(8,128)(2,1)} %bitcast.109, pred[16,128]{1,0:T(8,128)(4,1)S(1)} %compare_and_fusion), kind=kLoop, calls=%fused_computation.23 | loop fusion | flops 1572864 | bytes 6293504 | tf_op jit(solution)/shard_map/jit(_take)/select_n | solution.py:54
  221.7 6.9 %all-to-all-start.1 = ((bf16[16,128,768]{2,1,0:T(8,128)(2,1)}), bf16[16,128,768]{2,1,0:T(8,128)(2,1)}, u32[]{:S(2)}, u32[]{:S(2)}) async-start(bf16[16,128,768]{2,1,0:T(8,128)(2,1)} %broadcast_select_fusion.1), calls=%async_computation.1 | async-start | bytes 6291456 | tf_op jit(solution)/shard_map/all_to_all | solution.py:55
  229.2 8.6 %gather_fusion.4 = f32[1024]{0:T(1024)S(1)} fusion(f32[512,64]{0,1:T(8,128)S(1)} %fusion.27, s32[1024]{0:T(1024)S(1)} %reshape.389), kind=kCustom, calls=%fused_computation.4 | custom fusion | bytes 16384 | tf_op jit(solution)/shard_map/jit(take_along_axis)/gather | solution.py:58
  239.1 60.3 %all-to-all-done.1 = bf16[16,128,768]{2,1,0:T(8,128)(2,1)} async-done(((bf16[16,128,768]{2,1,0:T(8,128)(2,1)}), bf16[16,128,768]{2,1,0:T(8,128)(2,1)}, u32[]{:S(2)}, u32[]{:S(2)}) %all-to-all-start.1) | async-done | bytes 3145760 | tf_op jit(solution)/shard_map/all_to_all | solution.py:55
  299.4 7.8 %gather_fusion.3 = bf16[1024,768]{1,0:T(8,128)(2,1)} fusion(bf16[2048,768]{1,0:T(8,128)(2,1)} %bitcast.80, s32[1024]{0:T(1024)S(1)} %broadcast_clamp_fusion.1), kind=kCustom, calls=%fused_computation.3 | custom fusion | bytes 3149824 | tf_op jit(solution)/shard_map/jit(_take)/gather | solution.py:57
  307.2 3.6 %reshape.382 = bf16[512,2,768]{2,1,0:T(2,128)(2,1)S(1)} reshape(bf16[1024,768]{1,0:T(8,128)(2,1)} %gather_fusion.3) | data formatting | bytes 3145728 | tf_op jit(solution)/shard_map/jit(_take)/gather | solution.py:57
  310.8 6.5 %multiply_reduce_fusion = f32[512,768]{1,0:T(8,128)S(1)} fusion(bf16[512,2,768]{2,1,0:T(2,128)(2,1)S(1)} %reshape.382, pred[512,2]{1,0:T(8,128)(4,1)S(1)} %copy.25, f32[512,2]{1,0:T(8,128)S(1)} %copy.21), kind=kLoop, calls=%fused_computation.21 | loop fusion | flops 2752512 | bytes 3150848 | tf_op jit(solution)/shard_map/reduce_sum | solution.py:59
  317.3 1.1 add_convert_fusion
  (65 shorter events, 6.5 us)
Async XLA Ops:
  2.8 46.0 %copy-start.3 = (s32[512,64]{0,1:T(8,128)}, s32[512,64]{0,1:T(8,128)S(1)}, u32[]{:S(2)}) copy-start(s32[512,64]{0,1:T(8,128)S(1)} %get-tuple-element.9) | copy-start | bytes 393220
  48.5 45.2 %copy-start = (bf16[512,768]{1,0:T(8,128)(2,1)S(1)}, bf16[512,768]{1,0:T(8,128)(2,1)}, u32[]{:S(2)}) copy-start(bf16[512,768]{1,0:T(8,128)(2,1)} %param.4) | copy-start | bytes 2359300
  106.4 78.5 %all-to-all-start = ((bf16[16,128,768]{2,1,0:T(8,128)(2,1)}), bf16[16,128,768]{2,1,0:T(8,128)(2,1)}, u32[]{:S(2)}, u32[]{:S(2)}) async-start(bf16[16,128,768]{2,1,0:T(8,128)(2,1)} %broadcast_select_fusion), calls=%async_computation | async-start | bytes 6291456 | tf_op jit(solution)/shard_map/all_to_all | solution.py:34
  221.7 7.4 %copy-start.2 = (f32[512,64]{0,1:T(8,128)S(1)}, f32[512,64]{0,1:T(8,128)}, u32[]{:S(2)}) copy-start(f32[512,64]{0,1:T(8,128)} %param.5) | copy-start | bytes 393220
  221.7 77.7 %all-to-all-start.1 = ((bf16[16,128,768]{2,1,0:T(8,128)(2,1)}), bf16[16,128,768]{2,1,0:T(8,128)(2,1)}, u32[]{:S(2)}, u32[]{:S(2)}) async-start(bf16[16,128,768]{2,1,0:T(8,128)(2,1)} %broadcast_select_fusion.1), calls=%async_computation.1 | async-start | bytes 6291456 | tf_op jit(solution)/shard_map/all_to_all | solution.py:55
  307.2 10.1 %copy-start.1 = (bf16[512,768]{1,0:T(8,128)(2,1)S(1)}, bf16[512,768]{1,0:T(8,128)(2,1)}, u32[]{:S(2)}) copy-start(bf16[512,768]{1,0:T(8,128)(2,1)} %param.4) | copy-start | bytes 2359300
where the time goes:
time: 320 us; the launch traced here: 318 us
  waiting for transfers between devices  131 us (41%)
  local copies, waits for them, and re-layouts  65.6 us (20%)
  other arithmetic  60.8 us (19%)
  blocking collectives  28.8 us (9%)
  matrix products  17.2 us (5%)
  starting transfers between devices  14.1 us (4%)
    all_to_all x1, waiting for transfers between devices, local_step(): recv_buf = lax.all_to_all(send_buf, 'ep', 0, 0, tiled=True)  70.6 us
    all_to_all x1, waiting for transfers between devices, local_step(): ret_buf = lax.all_to_all(back_buf, 'ep', 0, 0, tiled=True)  60.3 us
    and x1, other arithmetic, local_step(): rows_back = jnp.take(ret_buf, send_row, axis=0, mode='fill', fill_value=0)  40 us
    unnamed x1, blocking collectives  28.8 us
    dot_general x1, matrix products, local_step(): jnp.einsum('ecf,efd->ecd', hidden, w_out, preferred_element_type=jnp.floa...  17.2 us
    gather x2, local copies, waits for them, and re-layouts, local_step(): rows_back = jnp.take(ret_buf, send_row, axis=0, mode='fill', fill_value=0)  11.4 us
    gather x1, local copies, waits for them, and re-layouts, local_step(): send_buf = jnp.take(x_rows, slot_tok, axis=0, mode='fill', fill_value=0)  9.44 us
    gather x1, local copies, waits for them, and re-layouts, local_step(): jnp.take(expert_out, back_row.reshape(-1), axis=0, mode='fill', fill_valu...  9.38 us
  transfers between devices with their start and end apart: 2, of which 2 were waited for; matrix products, arithmetic and copies ran while one was open for 4% of the time, Pallas kernels for 0%

commit v1 on v0

v1 whole, which is shorter than its diff:
```python
import functools

import jax
import jax.numpy as jnp
from jax import lax
from jax.experimental import pallas as pl
from jax.experimental.pallas import tpu as pltpu
from jax.sharding import PartitionSpec as P

CAP_FACTOR = 2
HOP_ROWS = (512, 512, 512, 512)
FF_TILE = 512
BF = jnp.bfloat16
F32 = jnp.float32
MESH = pl.DeviceIdType.MESH


def top_two(vals, axis):
    best = jnp.max(vals, axis=axis, keepdims=True)
    first = vals == best
    rest = jnp.where(first, -jnp.inf, vals)
    runner = jnp.max(rest, axis=axis, keepdims=True)
    return best, runner, first, rest == runner


def as_one(mask):
    return jnp.where(mask, 1.0, 0.0)


def iota_f(shape, dim):
    return lax.broadcasted_iota(jnp.int32, shape, dim).astype(F32)


def dot(lhs, rhs):
    return jnp.dot(lhs, rhs, preferred_element_type=F32)


def moe_kernel(n_ep, n_dp, capacity, src_cap, x_ref, lg_ref, w1_hbm, w2_hbm, out_ref, flag_ref,
               w1_buf, w2_buf, blk, ring, mirror, px, meta_send, metas, acc, z_acc, skey, rkeys,
               ret, back, y_acc, flag_buf,
               w_sem, send_sem, recv_sem, mir_send, mir_recv, px_sem, meta_ssem, meta_rsem,
               ret_ssem, ret_rsem, flag_ssem, flag_rsem):
    tok, d_model = x_ref.shape
    experts = lg_ref.shape[1]
    exp_dev = experts // n_ep
    ff = w1_buf.shape[2]
    n_chip = n_ep // 2
    half = n_chip // 2
    me = lax.axis_index('ep')
    my_dp = lax.axis_index('dp')
    chip = lax.div(me, 2)
    core = lax.rem(me, 2)
    other = chip * 2 + 1 - core
    nxt = (lax.rem(chip + 1, n_chip) * 2 + core, lax.rem(chip + n_chip - 1, n_chip) * 2 + core)
    bounds = (0,) + HOP_ROWS[::-1]
    starts = [sum(HOP_ROWS[:h]) for h in range(half)]

    def weight_copies(el):
        slot = el % 2
        return (pltpu.make_async_copy(w1_hbm.at[el], w1_buf.at[slot], w_sem.at[slot, 0]),
                pltpu.make_async_copy(w2_hbm.at[el], w2_buf.at[slot], w_sem.at[slot, 1]))

    for el in range(min(2, exp_dev)):
        for copy in weight_copies(el):
            copy.start()

    barrier = pltpu.get_barrier_semaphore()
    for step in range(1, n_ep):
        pl.semaphore_signal(barrier, inc=1, device_id={'ep': lax.rem(me + step, n_ep)}, device_id_type=MESH)
    for step in range(1, n_dp):
        pl.semaphore_signal(barrier, inc=1, device_id={'dp': lax.rem(my_dp + step, n_dp)}, device_id_type=MESH)

    logits = lg_ref[...]
    logits_t = logits.T
    _, _, first_t, second_t = top_two(logits_t, 0)
    row_i = lax.broadcasted_iota(jnp.int32, (tok, tok), 0)
    col_i = lax.broadcasted_iota(jnp.int32, (tok, tok), 1)
    upper = as_one(row_i < col_i).astype(BF)
    rank_t = dot(as_one(first_t | second_t).astype(BF), upper)
    e_ids = iota_f((experts, tok), 0)
    ranks, ids = [], []
    for mask in (first_t, second_t):
        ids.append(jnp.sum(jnp.where(mask, e_ids, 0.0), axis=0, keepdims=True))
        ranks.append(jnp.sum(jnp.where(mask, rank_t, 0.0), axis=0, keepdims=True))
    chip_f = chip.astype(F32)
    base = me.astype(F32) * float(experts * src_cap)
    reach = [jnp.zeros((1, tok), F32), jnp.zeros((1, tok), F32)]
    opposite = jnp.zeros((1, tok), jnp.bool_)
    for expert_id in ids:
        delta = jnp.floor((expert_id + 0.5) * (1.0 / (2 * exp_dev))) - chip_f
        delta = jnp.where(delta < 0.0, delta + n_chip, delta)
        reach[0] = jnp.maximum(reach[0], jnp.where(delta < half, delta, 0.0))
        reach[1] = jnp.maximum(reach[1], jnp.where(delta > half, n_chip - delta, 0.0))
        opposite = opposite | (delta == half)
    odd = lax.rem(lax.broadcasted_iota(jnp.int32, (1, tok), 1) + core, 2) == 0
    forward = (reach[0] > reach[1]) | ((reach[0] == reach[1]) & odd)
    reach = [jnp.where(opposite & forward, float(half), reach[0]),
             jnp.where(opposite & jnp.logical_not(forward), float(half), reach[1])]

    zero_row = jnp.zeros((1, tok), F32)
    info = jnp.concatenate([ids[0], ranks[0], ids[1], ranks[1], zero_row + 1.0, zero_row, zero_row, zero_row], axis=0).astype(BF)
    over = jnp.zeros((1, 1), F32)
    meta_send[...] = jnp.zeros_like(meta_send)
    x_val = x_ref[...]
    for way in range(2):
        level = float(half) - iota_f((8, tok), 0)
        member = as_one((reach[way] == level) & (level > 0.5))
        inner = dot(member.astype(BF), upper)
        sizes = jnp.sum(member, axis=1, keepdims=True)
        place = zero_row - 1.0
        total = jnp.zeros((1, 1), F32)
        for lev in range(half):
            place = jnp.where(member[lev:lev + 1] > 0.5, inner[lev:lev + 1] + total, place)
            total = total + sizes[lev:lev + 1]
            over = jnp.maximum(over, as_one(total > float(bounds[lev + 1])))
        pick = as_one(iota_f((HOP_ROWS[0], tok), 0) == place).astype(BF)
        blk[way] = dot(pick, x_val).astype(BF)
        keys = lax.dot_general(info, pick, (((1,), (1,)), ((), ())), preferred_element_type=F32)
        for c in range(2):
            key = base + keys[2 * c:2 * c + 1] * float(src_cap) + keys[2 * c + 1:2 * c + 2]
            meta_send[2 * way + c:2 * way + c + 1, 0:HOP_ROWS[0]] = jnp.where(keys[4:5] > 0.5, key, -1.0)
    for c in range(2):
        meta_send[6 + c:7 + c, :] = base + ids[c] * float(src_cap) + ranks[c]

    best, runner, first, second = top_two(logits, 1)
    chosen = as_one(first | second)
    meta_send[4:5, 0:experts] = jnp.sum(chosen, axis=0, keepdims=True)
    meta_send[5:6, :] = zero_row + over
    metas[me] = meta_send[...]
    rank = dot(as_one(row_i > col_i).astype(BF), chosen.astype(BF))
    lane_e = iota_f((tok, experts), 1)
    norm = jnp.sum(jnp.exp(logits - best), axis=1, keepdims=True)
    gates = (1.0 / norm, jnp.exp(runner - best) / norm)
    tkeys = [jnp.sum(jnp.where(mask, lane_e * float(src_cap) + rank, 0.0), axis=1, keepdims=True) for mask in (first, second)]

    pl.semaphore_wait(barrier, n_ep - 1 + n_dp - 1)

    def meta_copy(step):
        dest = lax.rem(me + step, n_ep)
        return pltpu.make_async_remote_copy(
            src_ref=meta_send, dst_ref=metas.at[me], send_sem=meta_ssem.at[step], recv_sem=meta_rsem.at[step],
            device_id={'ep': dest}, device_id_type=MESH)

    def hop_copy(way, hop, part):
        lo, size = bounds[part], bounds[part + 1] - bounds[part]
        src = blk.at[way, pl.ds(lo, size)] if hop == 0 else ring.at[way, pl.ds(starts[hop - 1] + lo, size)]
        return pltpu.make_async_remote_copy(
            src_ref=src, dst_ref=ring.at[way, pl.ds(starts[hop] + lo, size)],
            send_sem=send_sem.at[way, hop, part], recv_sem=recv_sem.at[way, hop, part],
            device_id={'ep': nxt[way]}, device_id_type=MESH)

    def mirror_copy(way, hop):
        rows = pl.ds(starts[hop], HOP_ROWS[hop])
        return pltpu.make_async_remote_copy(
            src_ref=ring.at[way, rows], dst_ref=mirror.at[way, rows],
            send_sem=mir_send.at[way, hop], recv_sem=mir_recv.at[way, hop],
            device_id={'ep': other}, device_id_type=MESH)

    px_copy = pltpu.make_async_remote_copy(
        src_ref=x_ref, dst_ref=px, send_sem=px_sem.at[0], recv_sem=px_sem.at[1],
        device_id={'ep': other}, device_id_type=MESH)

    def parts_of(hop):
        return [p for p in range(half - hop) if bounds[p + 1] > bounds[p]]

    px_copy.start()
    for step in range(1, n_ep):
        meta_copy(step).start()
    for part in parts_of(0):
        for way in range(2):
            hop_copy(way, 0, part).start()

    for step in range(1, n_ep):
        meta_copy(step).wait_recv()
    counts = jnp.concatenate([metas[s, 4:5, 0:experts] for s in range(n_ep)], axis=0)
    over = metas[0, 5:6, 0:128]
    for s in range(1, n_ep):
        over = jnp.maximum(over, metas[s, 5:6, 0:128])
    tri = as_one(lax.broadcasted_iota(jnp.int32, (n_ep, n_ep), 1) <= lax.broadcasted_iota(jnp.int32, (n_ep, n_ep), 0)).astype(BF)
    ends = dot(tri, counts.astype(BF))
    lane_ep = lax.broadcasted_iota(jnp.int32, (n_ep, experts), 1)
    slot = iota_f((n_ep, capacity), 1)
    for el in range(exp_dev):
        mine = lane_ep == me * exp_dev + el
        count_col = jnp.sum(jnp.where(mine, counts, 0.0), axis=1, keepdims=True)
        end_col = jnp.sum(jnp.where(mine, ends, 0.0), axis=1, keepdims=True)
        past = as_one(end_col <= slot)
        src = jnp.sum(past, axis=0, keepdims=True)
        rnk = slot[0:1] - jnp.sum(past * count_col, axis=0, keepdims=True)
        valid = src < float(n_ep)
        e_base = (me * exp_dev + el).astype(F32) * float(src_cap)
        key = jnp.where(valid, src * float(experts * src_cap) + e_base + rnk, -2.0)
        skey[el] = jnp.broadcast_to(key, (128, capacity)).T
        rkeys[el:el + 1, :] = jnp.where(valid, src * float(src_cap) + rnk, -1.0)

    def gather_rows(rows, keys_one, keys_two, first_time=False):
        def body(el, carry):
            want = skey[el][:, 0:1]
            hit = as_one((want == keys_one) | (want == keys_two)).astype(BF)
            part = dot(hit, rows[...])
            if first_time:
                acc[el] = part
            else:
                acc[el] = acc[el] + part
            return carry
        lax.fori_loop(0, exp_dev, body, 0)

    def gather_block(buf, way, hop, core_id):
        far = lax.rem(chip + (n_chip - 1 - hop if way == 0 else hop + 1), n_chip)
        src = far * 2 + core_id
        size = HOP_ROWS[hop]
        gather_rows(buf.at[way, pl.ds(starts[hop], size)],
                    metas[src, 2 * way:2 * way + 1, 0:size], metas[src, 2 * way + 1:2 * way + 2, 0:size])

    gather_rows(x_ref, metas[me, 6:7, :], metas[me, 7:8, :], True)
    px_copy.wait_recv()
    gather_rows(px, metas[other, 6:7, :], metas[other, 7:8, :])

    for hop in range(half):
        parts = parts_of(hop)
        for part in parts:
            for way in range(2):
                hop_copy(way, hop, part).wait_recv()
                if hop + 1 < half and part in parts_of(hop + 1):
                    hop_copy(way, hop + 1, part).start()
        for way in range(2):
            mirror_copy(way, hop).start()
        if hop > 0:
            for way in range(2):
                mirror_copy(way, hop - 1).wait_recv()
                gather_block(mirror, way, hop - 1, 1 - core)
        for way in range(2):
            gather_block(ring, way, hop, core)
    for way in range(2):
        mirror_copy(way, half - 1).wait_recv()
        gather_block(mirror, way, half - 1, 1 - core)

    flag_buf[0] = jnp.broadcast_to(over, (8, 128))

    def flag_copy(step):
        return pltpu.make_async_remote_copy(
            src_ref=flag_buf.at[0], dst_ref=flag_buf.at[step], send_sem=flag_ssem.at[step], recv_sem=flag_rsem.at[step],
            device_id={'dp': lax.rem(my_dp + step, n_dp)}, device_id_type=MESH)

    for step in range(1, n_dp):
        flag_copy(step).start()

    def ret_copy(el, step):
        dest = lax.rem(me + step, n_ep)
        return pltpu.make_async_remote_copy(
            src_ref=ret.at[el, pl.ds(pl.multiple_of(dest * src_cap, src_cap), src_cap)],
            dst_ref=back.at[el, pl.ds(pl.multiple_of(me * src_cap, src_cap), src_cap)],
            send_sem=ret_ssem.at[el, step], recv_sem=ret_rsem.at[el, step],
            device_id={'ep': dest}, device_id_type=MESH)

    ret_order = sorted(range(1, n_ep), key=lambda s: -min(s, n_ep - s))

    for el in range(exp_dev):
        for copy in weight_copies(el):
            copy.wait()
        rows = acc[el].astype(BF)
        z_acc[...] = jnp.zeros_like(z_acc)

        def ff_body(tile, carry, rows=rows, spot=el % 2):
            cols = pl.ds(pl.multiple_of(tile * FF_TILE, FF_TILE), FF_TILE)
            hidden = jax.nn.gelu(dot(rows, w1_buf[spot, :, cols]), approximate=True).astype(BF)
            z_acc[...] += dot(hidden, w2_buf[spot, cols, :])
            return carry

        lax.fori_loop(0, ff // FF_TILE, ff_body, 0)
        if el + 2 < exp_dev:
            for copy in weight_copies(el + 2):
                copy.start()
        spread = as_one(iota_f((n_ep * src_cap, capacity), 0) == rkeys[el:el + 1, :]).astype(BF)
        ret[el] = dot(spread, z_acc[...].astype(BF)).astype(BF)
        for step in ret_order:
            ret_copy(el, step).start()
        own = pl.ds(pl.multiple_of(me * src_cap, src_cap), src_cap)
        back[el, own, :] = ret[el, own, :]

    slot_i = lax.broadcasted_iota(jnp.int32, (1, n_ep * src_cap), 1)
    slot_src = lax.div(slot_i, src_cap)
    for el in range(exp_dev):
        for step in ret_order:
            ret_copy(el, step).wait_recv()
        slot_key = ((slot_src * exp_dev + el) * src_cap + (slot_i - slot_src * src_cap)).astype(F32)
        for c in range(2):
            hit = as_one(tkeys[c] == slot_key).astype(BF)
            part = gates[c] * dot(hit, back[el])
            if el == 0 and c == 0:
                y_acc[...] = part
            else:
                y_acc[...] += part
    out_ref[...] = (x_ref[...].astype(F32) + y_acc[...]).astype(BF)

    worst = flag_buf[0]
    for step in range(1, n_dp):
        flag_copy(step).wait_recv()
        worst = jnp.maximum(worst, flag_buf[step])
    flag_ref[...] = worst

    px_copy.wait_send()
    for step in range(1, n_ep):
        meta_copy(step).wait_send()
    for step in range(1, n_dp):
        flag_copy(step).wait_send()
    for hop in range(half):
        for way in range(2):
            mirror_copy(way, hop).wait_send()
            for part in parts_of(hop):
                hop_copy(way, hop, part).wait_send()
    for el in range(exp_dev):
        for step in ret_order:
            ret_copy(el, step).wait_send()


def solution(mesh):
    n_ep = mesh.shape['ep']
    n_dp = mesh.shape['dp']
    row_spec = P(('dp', 'ep'), None)
    expert_spec = P('ep', None, None)

    def local_step(x_rows, logits, w_in, w_out):
        tok, d_model = x_rows.shape
        experts = logits.shape[1]
        exp_dev, _, ff = w_in.shape
        capacity = CAP_FACTOR * tok * n_ep // experts
        src_cap = 4 * tok // experts
        half = n_ep // 4
        all_rows = sum(HOP_ROWS)
        vmem = pl.BlockSpec(memory_space=pltpu.VMEM)
        hbm = pl.BlockSpec(memory_space=pl.ANY)
        dma = pltpu.SemaphoreType.DMA
        out, flag = pl.pallas_call(
            functools.partial(moe_kernel, n_ep, n_dp, capacity, src_cap),
            out_shape=(jax.ShapeDtypeStruct((tok, d_model), BF), jax.ShapeDtypeStruct((8, 128), F32)),
            in_specs=[vmem, vmem, hbm, hbm],
            out_specs=(vmem, vmem),
            scratch_shapes=[
                pltpu.VMEM((2, d_model, ff), BF),
                pltpu.VMEM((2, ff, d_model), BF),
                pltpu.VMEM((2, HOP_ROWS[0], d_model), BF),
                pltpu.VMEM((2, all_rows, d_model), BF),
                pltpu.VMEM((2, all_rows, d_model), BF),
                pltpu.VMEM((tok, d_model), BF),
                pltpu.VMEM((8, tok), F32),
                pltpu.VMEM((n_ep, 8, tok), F32),
                pltpu.VMEM((exp_dev, capacity, d_model), F32),
                pltpu.VMEM((capacity, d_model), F32),
                pltpu.VMEM((exp_dev, capacity, 128), F32),
                pltpu.VMEM((8, capacity), F32),
                pltpu.VMEM((exp_dev, n_ep * src_cap, d_model), BF),
                pltpu.VMEM((exp_dev, n_ep * src_cap, d_model), BF),
                pltpu.VMEM((tok, d_model), F32),
                pltpu.VMEM((n_dp, 8, 128), F32),
                dma((2, 2)),
                dma((2, half, half)), dma((2, half, half)),
                dma((2, half)), dma((2, half)),
                dma((2,)),
                dma((n_ep,)), dma((n_ep,)),
                dma((exp_dev, n_ep)), dma((exp_dev, n_ep)),
                dma((n_dp,)), dma((n_dp,)),
            ],
            compiler_params=pltpu.CompilerParams(
                collective_id=0, has_side_effects=True, vmem_limit_bytes=62 * 1024 * 1024),
            name='moe_layer',
        )(x_rows, logits, w_in, w_out)
        return out

    return jax.shard_map(local_step, mesh=mesh, in_specs=(row_spec, row_spec, expert_spec, expert_spec), out_specs=row_spec, check_vma=False)
```

time: 320 us -> 181 us (0.57)
  Pallas kernels: 0 us -> 176 us
  waiting for transfers between devices: 131 us -> 0 us
  local copies, waits for them, and re-layouts: 65.6 us -> 3.8 us
  other arithmetic: 60.8 us -> 0 us
  blocking collectives: 28.8 us -> 0 us
  matrix products: 17.2 us -> 0 us
  starting transfers between devices: 14.1 us -> 0 us
    pallas_call x0 -> x1, Pallas kernels: none -> 176 us  [local_step(): pl.pallas_call(functools.partial(moe_kernel, n_ep, n_dp, capacity, src_ca...]
    all_to_all x2 -> x0, waiting for transfers between devices: 131 us -> none  [the longest x1 70.6 us: local_step(): recv_buf = lax.all_to_all(send_buf, 'ep', 0, 0, tiled=True)]
    gather x17 -> x0, local copies, waits for them, and re-layouts: 58.1 us -> none  [the longest x2 11.4 us: local_step(): rows_back = jnp.take(ret_buf, send_row, axis=0, mode='fill', fill_value=0)]
    and x3 -> x0, other arithmetic: 40 us -> none  [the longest x1 40 us: local_step(): rows_back = jnp.take(ret_buf, send_row, axis=0, mode='fill', fill_value=0)]
    unnamed x1 -> x0, blocking collectives: 28.8 us -> none
    dot_general x1 -> x0, matrix products: 17.2 us -> none  [local_step(): jnp.einsum('ecf,efd->ecd', hidden, w_out, preferred_element_type=jnp.floa...]
    all_to_all x2 -> x0, starting transfers between devices: 14.1 us -> none  [the longest x1 7.22 us: local_step(): recv_buf = lax.all_to_all(send_buf, 'ep', 0, 0, tiled=True)]
    reduce_sum x4 -> x0, other arithmetic: 7.74 us -> none  [the longest x1 6.51 us: local_step(): jnp.sum(pick_gate[:, :, None] * rows_back.astype(jnp.float32), axis=1)]
  transfers between devices with their start and end apart: 2 -> 0, of which waited for: 2 -> 0; matrix products, arithmetic and copies ran while one was open for 4% -> 0% of each run, Pallas kernels for 0% -> 0%
where the time goes in v1:
time: 181 us; the launch traced here: 180 us
  Pallas kernels  176 us (97%)
  local copies, waits for them, and re-layouts  3.8 us (2%)
    pallas_call x1, Pallas kernels, local_step(): pl.pallas_call(functools.partial(moe_kernel, n_ep, n_dp, capacity, src_ca...  176 us
    unnamed x2, local copies, waits for them, and re-layouts  3.8 us

profile of v1, /device:TPU:21, one launch (start us, length us, event | category | flops | bytes accessed | tf_op | source)
XLA Modules:
  0.0 179.7 jit_solution(4166759348799441694)
XLA Ops:
  0.0 1.7 copy.5.lg_ref
  1.7 175.9 %moe_layer.1 = (bf16[512,768]{1,0:T(8,128)(2,1)}, f32[8,128]{1,0:T(8,128)}) custom-call(bf16[512,768]{1,0:T(8,128)(2,1)} %x_ref.1, f32[512,64]{1,0:T(8,128)} %copy.5.lg_ref, bf16[4,768,3072]{2,1,0:T(8,128)(2,1)} %w1_hbm.1, bf16[4,3072,768]{2,1,0:T(8,128)(2,1)} %w2_hbm.1), custom_call_target="tpu_custom_call" | custom-call | tf_op jit(solution)/shard_map/moe_layer/pallas_call | solution.py:334
  177.7 2.1 %copy.7 = bf16[512,768]{1,0:T(8,128)(2,1)} copy(bf16[512,768]{1,0:T(8,128)(2,1)} %get-tuple-element.6) | data formatting | bytes 1572864

commit v2 on v1

--- a/solution.py
+++ b/solution.py
@@ -8,7 +8,7 @@
 from jax.sharding import PartitionSpec as P
 
 CAP_FACTOR = 2
-HOP_ROWS = (512, 512, 512, 512)
+HOP_ROWS = (464, 384, 304, 160)
 FF_TILE = 512
 BF = jnp.bfloat16
 F32 = jnp.float32
@@ -56,7 +56,7 @@
     starts = [sum(HOP_ROWS[:h]) for h in range(half)]
 
     def weight_copies(el):
-        slot = el % 2
+        slot = lax.rem(el, 2)
         return (pltpu.make_async_copy(w1_hbm.at[el], w1_buf.at[slot], w_sem.at[slot, 0]),
                 pltpu.make_async_copy(w2_hbm.at[el], w2_buf.at[slot], w_sem.at[slot, 1]))
 
@@ -255,42 +255,50 @@
 
     ret_order = sorted(range(1, n_ep), key=lambda s: -min(s, n_ep - s))
 
-    for el in range(exp_dev):
+    def expert_body(el, carry):
+        spot = lax.rem(el, 2)
         for copy in weight_copies(el):
             copy.wait()
         rows = acc[el].astype(BF)
         z_acc[...] = jnp.zeros_like(z_acc)
 
-        def ff_body(tile, carry, rows=rows, spot=el % 2):
+        def ff_body(tile, inner):
             cols = pl.ds(pl.multiple_of(tile * FF_TILE, FF_TILE), FF_TILE)
             hidden = jax.nn.gelu(dot(rows, w1_buf[spot, :, cols]), approximate=True).astype(BF)
             z_acc[...] += dot(hidden, w2_buf[spot, cols, :])
-            return carry
+            return inner
 
         lax.fori_loop(0, ff // FF_TILE, ff_body, 0)
-        if el + 2 < exp_dev:
+
+        @pl.when(el + 2 < exp_dev)
+        def _():
             for copy in weight_copies(el + 2):
                 copy.start()
-        spread = as_one(iota_f((n_ep * src_cap, capacity), 0) == rkeys[el:el + 1, :]).astype(BF)
+
+        spread = as_one(iota_f((n_ep * src_cap, capacity), 0) == rkeys[pl.ds(el, 1), :]).astype(BF)
         ret[el] = dot(spread, z_acc[...].astype(BF)).astype(BF)
         for step in ret_order:
             ret_copy(el, step).start()
         own = pl.ds(pl.multiple_of(me * src_cap, src_cap), src_cap)
         back[el, own, :] = ret[el, own, :]
+        return carry
+
+    lax.fori_loop(0, exp_dev, expert_body, 0)
 
     slot_i = lax.broadcasted_iota(jnp.int32, (1, n_ep * src_cap), 1)
     slot_src = lax.div(slot_i, src_cap)
-    for el in range(exp_dev):
+    y_acc[...] = jnp.zeros_like(y_acc)
+
+    def mix_body(el, carry):
         for step in ret_order:
             ret_copy(el, step).wait_recv()
         slot_key = ((slot_src * exp_dev + el) * src_cap + (slot_i - slot_src * src_cap)).astype(F32)
         for c in range(2):
             hit = as_one(tkeys[c] == slot_key).astype(BF)
-            part = gates[c] * dot(hit, back[el])
-            if el == 0 and c == 0:
-                y_acc[...] = part
-            else:
-                y_acc[...] += part
+            y_acc[...] += gates[c] * dot(hit, back[el])
+        return carry
+
+    lax.fori_loop(0, exp_dev, mix_body, 0)
     out_ref[...] = (x_ref[...].astype(F32) + y_acc[...]).astype(BF)
 
     worst = flag_buf[0]
@@ -312,6 +320,55 @@
     for el in range(exp_dev):
         for step in ret_order:
             ret_copy(el, step).wait_send()
+
+
+def plain_step(n_ep, x_rows, logits, w_in, w_out):
+    tok_dev, d_model = x_rows.shape
+    experts = logits.shape[1]
+    exp_dev = w_in.shape[0]
+    capacity = CAP_FACTOR * tok_dev * n_ep // experts
+    src_cap = 4 * tok_dev // experts
+    my_index = lax.axis_index('ep')
+    gate_probs = jax.nn.softmax(logits, axis=-1)
+    top_vals, top_ids = lax.top_k(logits, 2)
+    chosen = (logits >= top_vals[:, 1:2]).astype(jnp.int32)
+    local_before = jnp.cumsum(chosen, axis=0) - chosen
+    local_counts = jnp.sum(chosen, axis=0).astype(jnp.float32)
+    all_counts = lax.all_gather(local_counts, 'ep').astype(jnp.int32)
+    dev_offsets = jnp.cumsum(all_counts, axis=0) - all_counts
+    local_pos = jnp.take_along_axis(local_before, top_ids, axis=1)
+    kept_mask = local_pos + jnp.take(dev_offsets[my_index], top_ids) < capacity
+    send_row = jnp.where(kept_mask, top_ids * src_cap + local_pos, experts * src_cap)
+    tok_ids = jnp.broadcast_to(jnp.arange(tok_dev, dtype=jnp.int32)[:, None], (tok_dev, 2))
+    slot_tok = jnp.full((experts * src_cap,), tok_dev, jnp.int32).at[send_row.reshape(-1)].set(tok_ids.reshape(-1), mode='drop')
+    send_buf = jnp.take(x_rows, slot_tok, axis=0, mode='fill', fill_value=0)
+    recv_buf = lax.all_to_all(send_buf, 'ep', 0, 0, tiled=True)
+
+    own_counts = lax.dynamic_slice_in_dim(all_counts, my_index * exp_dev, exp_dev, axis=1)
+    own_offsets = lax.dynamic_slice_in_dim(dev_offsets, my_index * exp_dev, exp_dev, axis=1)
+    kept_counts = jnp.minimum(jnp.maximum(capacity - own_offsets, 0), own_counts)
+    slot_ends = (own_offsets + kept_counts).T
+    cap_ids = jnp.arange(capacity, dtype=jnp.int32)
+    below_mask = slot_ends[:, None, :] <= cap_ids[None, :, None]
+    src_dev = jnp.sum(below_mask.astype(jnp.int32), axis=2)
+    slot_start = jnp.sum(jnp.where(below_mask, kept_counts.T[:, None, :], 0), axis=2)
+    exp_local = jnp.arange(exp_dev, dtype=jnp.int32)
+    recv_row = (src_dev * exp_dev + exp_local[:, None]) * src_cap + cap_ids[None, :] - slot_start
+    recv_row = jnp.where(src_dev < n_ep, recv_row, n_ep * exp_dev * src_cap)
+    expert_rows = jnp.take(recv_buf, recv_row.reshape(-1), axis=0, mode='fill', fill_value=0).reshape(exp_dev, capacity, d_model)
+    hidden = jax.nn.gelu(jnp.einsum('ecd,edf->ecf', expert_rows, w_in, preferred_element_type=jnp.float32), approximate=True).astype(jnp.bfloat16)
+    expert_out = jnp.einsum('ecf,efd->ecd', hidden, w_out, preferred_element_type=jnp.float32).astype(jnp.bfloat16).reshape(exp_dev * capacity, d_model)
+
+    src_slots = jnp.arange(src_cap, dtype=jnp.int32)
+    back_row = exp_local[None, :, None] * capacity + own_offsets[:, :, None] + src_slots[None, None, :]
+    back_row = jnp.where(src_slots[None, None, :] < kept_counts[:, :, None], back_row, exp_dev * capacity)
+    back_buf = jnp.take(expert_out, back_row.reshape(-1), axis=0, mode='fill', fill_value=0)
+    ret_buf = lax.all_to_all(back_buf, 'ep', 0, 0, tiled=True)
+
+    rows_back = jnp.take(ret_buf, send_row, axis=0, mode='fill', fill_value=0)
+    pick_gate = jnp.take_along_axis(gate_probs, top_ids, axis=1)
+    mix_sum = jnp.sum(pick_gate[:, :, None] * rows_back.astype(jnp.float32), axis=1)
+    return (x_rows.astype(jnp.float32) + mix_sum).astype(jnp.bfloat16)
 
 
 def solution(mesh):
@@ -365,6 +422,6 @@
                 collective_id=0, has_side_effects=True, vmem_limit_bytes=62 * 1024 * 1024),
             name='moe_layer',
         )(x_rows, logits, w_in, w_out)
-        return out
+        return lax.cond(flag[0, 0] > 0.0, functools.partial(plain_step, n_ep), lambda *_: out, x_rows, logits, w_in, w_out)
 
     return jax.shard_map(local_step, mesh=mesh, in_specs=(row_spec, row_spec, expert_spec, expert_spec), out_specs=row_spec, check_vma=False)

time: 181 us -> 157 us (0.87)
  Pallas kernels: 176 us -> 151 us
    pallas_call x1, Pallas kernels: 176 us -> 151 us  [local_step(): pl.pallas_call(functools.partial(moe_kernel, n_ep, n_dp, capacity, src_ca...]
    unnamed x2 -> x6, local copies, waits for them, and re-layouts: 3.8 us -> 3.81 us
where the time goes in v2:
time: 157 us
  Pallas kernels  151 us (96%)
  local copies, waits for them, and re-layouts  5 us (3%)
    pallas_call x1, Pallas kernels, local_step(): pl.pallas_call(functools.partial(moe_kernel, n_ep, n_dp, capacity, src_ca...  151 us
    unnamed x6, local copies, waits for them, and re-layouts  3.81 us

profile of v2, /device:TPU:21, one launch (start us, length us, event | category | flops | bytes accessed | tf_op | source)
XLA Modules:
  0.0 156.8 jit_solution(649219074287603000)
XLA Ops:
  0.0 1.7 %copy.40.lg_ref = f32[512,64]{1,0:T(8,128)} copy(f32[512,64]{0,1:T(8,128)} %param.7) | data formatting | bytes 262144 | tf_op args[1]
  1.7 0.0 copy-start
  1.7 0.0 copy-start.5
  1.7 150.9 %moe_layer.1 = (bf16[512,768]{1,0:T(8,128)(2,1)}, f32[8,128]{1,0:T(8,128)}) custom-call(bf16[512,768]{1,0:T(8,128)(2,1)} %x_ref.1, f32[512,64]{1,0:T(8,128)} %copy.40.lg_ref, bf16[4,768,3072]{2,1,0:T(8,128)(2,1)} %w1_hbm.1, bf16[4,3072,768]{2,1,0:T(8,128)(2,1)} %w2_hbm.1), custom_call_target="tpu_custom_call" | custom-call | tf_op jit(solution)/shard_map/moe_layer/pallas_call | solution.py:391
  152.7 1.2 slice.15
  154.5 0.0 copy-done
  154.5 0.0 copy-done.5
  154.5 0.2 conditional.1
  154.8 2.1 %copy.50 = bf16[512,768]{1,0:T(8,128)(2,1)} copy(bf16[512,768]{1,0:T(8,128)(2,1)} %get-tuple-element.29) | data formatting | bytes 1572864
Async XLA Ops:
  1.7 152.8 %copy-start = (bf16[512,768]{1,0:T(8,128)(2,1)S(1)}, bf16[512,768]{1,0:T(8,128)(2,1)}, u32[]{:S(2)}) copy-start(bf16[512,768]{1,0:T(8,128)(2,1)} %x_ref.1) | copy-start | bytes 2359300
  1.7 152.8 %copy-start.5 = (f32[512,64]{0,1:T(8,128)S(1)}, f32[512,64]{0,1:T(8,128)}, u32[]{:S(2)}) copy-start(f32[512,64]{0,1:T(8,128)} %param.7) | copy-start | bytes 393220

commit v3 on v2

--- a/solution.py
+++ b/solution.py
@@ -36,12 +36,12 @@
 
 
 def moe_kernel(n_ep, n_dp, capacity, src_cap, x_ref, lg_ref, w1_hbm, w2_hbm, out_ref, flag_ref,
-               w1_buf, w2_buf, blk, ring, mirror, px, meta_send, metas, acc, z_acc, skey, rkeys,
-               ret, back, y_acc, flag_buf,
-               w_sem, send_sem, recv_sem, mir_send, mir_recv, px_sem, meta_ssem, meta_rsem,
-               ret_ssem, ret_rsem, flag_ssem, flag_rsem):
+               w1_buf, w2_buf, blk, near, hops_a, hops_b, hops_c, hops_d, key_send, key_near, key_ring, key_mir,
+               count_send, count_all, acc, z_acc, skey, rkeys, ret, back, y_acc, flag_buf,
+               w_sem, send_sem, recv_sem, mir_send, mir_recv, px_sem, ksend_sem, krecv_sem, kmir_send, kmir_recv,
+               kpx_sem, count_ssem, count_rsem, ret_ssem, ret_rsem, flag_ssem, flag_rsem):
     tok, d_model = x_ref.shape
-    experts = lg_ref.shape[1]
+    experts = lg_ref.shape[0]
     exp_dev = experts // n_ep
     ff = w1_buf.shape[2]
     n_chip = n_ep // 2
@@ -53,7 +53,7 @@
     other = chip * 2 + 1 - core
     nxt = (lax.rem(chip + 1, n_chip) * 2 + core, lax.rem(chip + n_chip - 1, n_chip) * 2 + core)
     bounds = (0,) + HOP_ROWS[::-1]
-    starts = [sum(HOP_ROWS[:h]) for h in range(half)]
+    hop_bufs = (hops_a, hops_b, hops_c, hops_d)
 
     def weight_copies(el):
         slot = lax.rem(el, 2)
@@ -70,8 +70,8 @@
     for step in range(1, n_dp):
         pl.semaphore_signal(barrier, inc=1, device_id={'dp': lax.rem(my_dp + step, n_dp)}, device_id_type=MESH)
 
-    logits = lg_ref[...]
-    logits_t = logits.T
+    logits_t = lg_ref[...]
+    logits = logits_t.T
     _, _, first_t, second_t = top_two(logits_t, 0)
     row_i = lax.broadcasted_iota(jnp.int32, (tok, tok), 0)
     col_i = lax.broadcasted_iota(jnp.int32, (tok, tok), 1)
@@ -100,8 +100,8 @@
     zero_row = jnp.zeros((1, tok), F32)
     info = jnp.concatenate([ids[0], ranks[0], ids[1], ranks[1], zero_row + 1.0, zero_row, zero_row, zero_row], axis=0).astype(BF)
     over = jnp.zeros((1, 1), F32)
-    meta_send[...] = jnp.zeros_like(meta_send)
     x_val = x_ref[...]
+    near[0:tok, :] = x_val
     for way in range(2):
         level = float(half) - iota_f((8, tok), 0)
         member = as_one((reach[way] == level) & (level > 0.5))
@@ -118,15 +118,16 @@
         keys = lax.dot_general(info, pick, (((1,), (1,)), ((), ())), preferred_element_type=F32)
         for c in range(2):
             key = base + keys[2 * c:2 * c + 1] * float(src_cap) + keys[2 * c + 1:2 * c + 2]
-            meta_send[2 * way + c:2 * way + c + 1, 0:HOP_ROWS[0]] = jnp.where(keys[4:5] > 0.5, key, -1.0)
+            key_send[way, c:c + 1, 0:HOP_ROWS[0]] = jnp.where(keys[4:5] > 0.5, key, -1.0)
     for c in range(2):
-        meta_send[6 + c:7 + c, :] = base + ids[c] * float(src_cap) + ranks[c]
+        key_near[0, c:c + 1, :] = base + ids[c] * float(src_cap) + ranks[c]
 
     best, runner, first, second = top_two(logits, 1)
     chosen = as_one(first | second)
-    meta_send[4:5, 0:experts] = jnp.sum(chosen, axis=0, keepdims=True)
-    meta_send[5:6, :] = zero_row + over
-    metas[me] = meta_send[...]
+    lanes = 128
+    count_send[...] = jnp.concatenate(
+        [jnp.sum(chosen, axis=0, keepdims=True), jnp.zeros((1, lanes - experts), F32) + over], axis=1)
+    count_all[me] = count_send[...]
     rank = dot(as_one(row_i > col_i).astype(BF), chosen.astype(BF))
     lane_e = iota_f((tok, experts), 1)
     norm = jnp.sum(jnp.exp(logits - best), axis=1, keepdims=True)
@@ -135,47 +136,57 @@
 
     pl.semaphore_wait(barrier, n_ep - 1 + n_dp - 1)
 
-    def meta_copy(step):
-        dest = lax.rem(me + step, n_ep)
+    def remote(src, dst, send, recv, to):
         return pltpu.make_async_remote_copy(
-            src_ref=meta_send, dst_ref=metas.at[me], send_sem=meta_ssem.at[step], recv_sem=meta_rsem.at[step],
-            device_id={'ep': dest}, device_id_type=MESH)
+            src_ref=src, dst_ref=dst, send_sem=send, recv_sem=recv, device_id=to, device_id_type=MESH)
+
+    def count_copy(step):
+        return remote(count_send, count_all.at[me], count_ssem.at[step], count_rsem.at[step],
+                      {'ep': lax.rem(me + step, n_ep)})
+
+    def ring_rows(way, hop, lo, size):
+        return hop_bufs[hop].at[pl.ds(way * HOP_ROWS[hop] + lo, size)]
 
     def hop_copy(way, hop, part):
         lo, size = bounds[part], bounds[part + 1] - bounds[part]
-        src = blk.at[way, pl.ds(lo, size)] if hop == 0 else ring.at[way, pl.ds(starts[hop - 1] + lo, size)]
-        return pltpu.make_async_remote_copy(
-            src_ref=src, dst_ref=ring.at[way, pl.ds(starts[hop] + lo, size)],
-            send_sem=send_sem.at[way, hop, part], recv_sem=recv_sem.at[way, hop, part],
-            device_id={'ep': nxt[way]}, device_id_type=MESH)
+        src = blk.at[way, pl.ds(lo, size)] if hop == 0 else ring_rows(way, hop - 1, lo, size)
+        return remote(src, ring_rows(way, hop, lo, size), send_sem.at[way, hop, part], recv_sem.at[way, hop, part],
+                      {'ep': nxt[way]})
+
+    def key_copy(way, hop):
+        src = key_send.at[way] if hop == 0 else key_ring.at[way, hop - 1]
+        return remote(src, key_ring.at[way, hop], ksend_sem.at[way, hop], krecv_sem.at[way, hop], {'ep': nxt[way]})
 
     def mirror_copy(way, hop):
-        rows = pl.ds(starts[hop], HOP_ROWS[hop])
-        return pltpu.make_async_remote_copy(
-            src_ref=ring.at[way, rows], dst_ref=mirror.at[way, rows],
-            send_sem=mir_send.at[way, hop], recv_sem=mir_recv.at[way, hop],
-            device_id={'ep': other}, device_id_type=MESH)
-
-    px_copy = pltpu.make_async_remote_copy(
-        src_ref=x_ref, dst_ref=px, send_sem=px_sem.at[0], recv_sem=px_sem.at[1],
-        device_id={'ep': other}, device_id_type=MESH)
+        return remote(ring_rows(way, hop, 0, HOP_ROWS[hop]), ring_rows(2 + way, hop, 0, HOP_ROWS[hop]),
+                      mir_send.at[way, hop], mir_recv.at[way, hop], {'ep': other})
+
+    def key_mirror(way, hop):
+        return remote(key_ring.at[way, hop], key_mir.at[way, hop], kmir_send.at[way, hop], kmir_recv.at[way, hop],
+                      {'ep': other})
+
+    px_copy = remote(x_ref, near.at[pl.ds(tok, tok)], px_sem.at[0], px_sem.at[1], {'ep': other})
+    kpx_copy = remote(key_near.at[0], key_near.at[1], kpx_sem.at[0], kpx_sem.at[1], {'ep': other})
 
     def parts_of(hop):
         return [p for p in range(half - hop) if bounds[p + 1] > bounds[p]]
 
+    for way in range(2):
+        hop_copy(way, 0, 0).start()
+    for step in range(1, n_ep):
+        count_copy(step).start()
     px_copy.start()
+    kpx_copy.start()
+    for way in range(2):
+        key_copy(way, 0).start()
+        for part in parts_of(0)[1:]:
+            hop_copy(way, 0, part).start()
+
     for step in range(1, n_ep):
-        meta_copy(step).start()
-    for part in parts_of(0):
-        for way in range(2):
-            hop_copy(way, 0, part).start()
-
-    for step in range(1, n_ep):
-        meta_copy(step).wait_recv()
-    counts = jnp.concatenate([metas[s, 4:5, 0:experts] for s in range(n_ep)], axis=0)
-    over = metas[0, 5:6, 0:128]
-    for s in range(1, n_ep):
-        over = jnp.maximum(over, metas[s, 5:6, 0:128])
+        count_copy(step).wait_recv()
+    count_rows = jnp.concatenate([count_all[s] for s in range(n_ep)], axis=0)
+    counts = count_rows[:, 0:experts]
+    over = jnp.max(jnp.max(count_rows[:, experts:lanes], axis=1, keepdims=True), axis=0, keepdims=True)
     tri = as_one(lax.broadcasted_iota(jnp.int32, (n_ep, n_ep), 1) <= lax.broadcasted_iota(jnp.int32, (n_ep, n_ep), 0)).astype(BF)
     ends = dot(tri, counts.astype(BF))
     lane_ep = lax.broadcasted_iota(jnp.int32, (n_ep, experts), 1)
@@ -193,47 +204,46 @@
         skey[el] = jnp.broadcast_to(key, (128, capacity)).T
         rkeys[el:el + 1, :] = jnp.where(valid, src * float(src_cap) + rnk, -1.0)
 
-    def gather_rows(rows, keys_one, keys_two, first_time=False):
+    def gather_rows(el, buf, keys, first_time=False):
+        want = skey[el][:, 0:1]
+        hit = as_one((want == keys[0:1]) | (want == keys[1:2])).astype(BF)
+        part = dot(hit, buf[...])
+        return part if first_time else acc[el] + part
+
+    def gather_all(buf, keys, first_time=False):
         def body(el, carry):
-            want = skey[el][:, 0:1]
-            hit = as_one((want == keys_one) | (want == keys_two)).astype(BF)
-            part = dot(hit, rows[...])
-            if first_time:
-                acc[el] = part
-            else:
-                acc[el] = acc[el] + part
+            acc[el] = gather_rows(el, buf, keys, first_time)
             return carry
         lax.fori_loop(0, exp_dev, body, 0)
 
-    def gather_block(buf, way, hop, core_id):
-        far = lax.rem(chip + (n_chip - 1 - hop if way == 0 else hop + 1), n_chip)
-        src = far * 2 + core_id
+    def hop_keys(hop):
+        for way in range(2):
+            mirror_copy(way, hop).wait_recv()
+            key_mirror(way, hop).wait_recv()
         size = HOP_ROWS[hop]
-        gather_rows(buf.at[way, pl.ds(starts[hop], size)],
-                    metas[src, 2 * way:2 * way + 1, 0:size], metas[src, 2 * way + 1:2 * way + 2, 0:size])
-
-    gather_rows(x_ref, metas[me, 6:7, :], metas[me, 7:8, :], True)
+        return jnp.concatenate([keys[way, hop][:, 0:size] for keys in (key_ring, key_mir) for way in range(2)], axis=1)
+
     px_copy.wait_recv()
-    gather_rows(px, metas[other, 6:7, :], metas[other, 7:8, :])
+    kpx_copy.wait_recv()
+    gather_all(near, jnp.concatenate([key_near[0], key_near[1]], axis=1), True)
 
     for hop in range(half):
-        parts = parts_of(hop)
-        for part in parts:
+        for part in parts_of(hop):
             for way in range(2):
                 hop_copy(way, hop, part).wait_recv()
-                if hop + 1 < half and part in parts_of(hop + 1):
+                onward = hop + 1 < half
+                if onward and part in parts_of(hop + 1):
                     hop_copy(way, hop + 1, part).start()
+                if part == 0:
+                    key_copy(way, hop).wait_recv()
+                    key_mirror(way, hop).start()
+                    if onward:
+                        key_copy(way, hop + 1).start()
         for way in range(2):
             mirror_copy(way, hop).start()
-        if hop > 0:
-            for way in range(2):
-                mirror_copy(way, hop - 1).wait_recv()
-                gather_block(mirror, way, hop - 1, 1 - core)
-        for way in range(2):
-            gather_block(ring, way, hop, core)
-    for way in range(2):
-        mirror_copy(way, half - 1).wait_recv()
-        gather_block(mirror, way, half - 1, 1 - core)
+        if hop + 1 < half:
+            gather_all(hop_bufs[hop], hop_keys(hop))
+    last_keys = hop_keys(half - 1)
 
     flag_buf[0] = jnp.broadcast_to(over, (8, 128))
 
@@ -259,7 +269,7 @@
         spot = lax.rem(el, 2)
         for copy in weight_copies(el):
             copy.wait()
-        rows = acc[el].astype(BF)
+        rows = gather_rows(el, hop_bufs[half - 1], last_keys).astype(BF)
         z_acc[...] = jnp.zeros_like(z_acc)
 
         def ff_body(tile, inner):
@@ -305,16 +315,19 @@
     for step in range(1, n_dp):
         flag_copy(step).wait_recv()
         worst = jnp.maximum(worst, flag_buf[step])
-    flag_ref[...] = worst
+    flag_ref[0] = jnp.max(worst)
 
     px_copy.wait_send()
+    kpx_copy.wait_send()
     for step in range(1, n_ep):
-        meta_copy(step).wait_send()
+        count_copy(step).wait_send()
     for step in range(1, n_dp):
         flag_copy(step).wait_send()
     for hop in range(half):
         for way in range(2):
             mirror_copy(way, hop).wait_send()
+            key_mirror(way, hop).wait_send()
+            key_copy(way, hop).wait_send()
             for part in parts_of(hop):
                 hop_copy(way, hop, part).wait_send()
     for el in range(exp_dev):
@@ -384,24 +397,27 @@
         capacity = CAP_FACTOR * tok * n_ep // experts
         src_cap = 4 * tok // experts
         half = n_ep // 4
-        all_rows = sum(HOP_ROWS)
         vmem = pl.BlockSpec(memory_space=pltpu.VMEM)
+        smem = pl.BlockSpec(memory_space=pltpu.SMEM)
         hbm = pl.BlockSpec(memory_space=pl.ANY)
         dma = pltpu.SemaphoreType.DMA
         out, flag = pl.pallas_call(
             functools.partial(moe_kernel, n_ep, n_dp, capacity, src_cap),
-            out_shape=(jax.ShapeDtypeStruct((tok, d_model), BF), jax.ShapeDtypeStruct((8, 128), F32)),
+            out_shape=(jax.ShapeDtypeStruct((tok, d_model), BF), jax.ShapeDtypeStruct((1,), F32)),
             in_specs=[vmem, vmem, hbm, hbm],
-            out_specs=(vmem, vmem),
+            out_specs=(vmem, smem),
             scratch_shapes=[
                 pltpu.VMEM((2, d_model, ff), BF),
                 pltpu.VMEM((2, ff, d_model), BF),
                 pltpu.VMEM((2, HOP_ROWS[0], d_model), BF),
-                pltpu.VMEM((2, all_rows, d_model), BF),
-                pltpu.VMEM((2, all_rows, d_model), BF),
-                pltpu.VMEM((tok, d_model), BF),
-                pltpu.VMEM((8, tok), F32),
-                pltpu.VMEM((n_ep, 8, tok), F32),
+                pltpu.VMEM((2 * tok, d_model), BF),
+                *[pltpu.VMEM((4 * rows, d_model), BF) for rows in HOP_ROWS],
+                pltpu.VMEM((2, 2, tok), F32),
+                pltpu.VMEM((2, 2, tok), F32),
+                pltpu.VMEM((2, half, 2, tok), F32),
+                pltpu.VMEM((2, half, 2, tok), F32),
+                pltpu.VMEM((1, 128), F32),
+                pltpu.VMEM((n_ep, 1, 128), F32),
                 pltpu.VMEM((exp_dev, capacity, d_model), F32),
                 pltpu.VMEM((capacity, d_model), F32),
                 pltpu.VMEM((exp_dev, capacity, 128), F32),
@@ -414,6 +430,8 @@
                 dma((2, half, half)), dma((2, half, half)),
                 dma((2, half)), dma((2, half)),
                 dma((2,)),
+                dma((2, half)), dma((2, half)), dma((2, half)), dma((2, half)),
+                dma((2,)),
                 dma((n_ep,)), dma((n_ep,)),
                 dma((exp_dev, n_ep)), dma((exp_dev, n_ep)),
                 dma((n_dp,)), dma((n_dp,)),
@@ -421,7 +439,7 @@
             compiler_params=pltpu.CompilerParams(
                 collective_id=0, has_side_effects=True, vmem_limit_bytes=62 * 1024 * 1024),
             name='moe_layer',
-        )(x_rows, logits, w_in, w_out)
-        return lax.cond(flag[0, 0] > 0.0, functools.partial(plain_step, n_ep), lambda *_: out, x_rows, logits, w_in, w_out)
+        )(x_rows, logits.T, w_in, w_out)
+        return lax.cond(flag[0] > 0.0, functools.partial(plain_step, n_ep), lambda *_: out, x_rows, logits, w_in, w_out)
 
     return jax.shard_map(local_step, mesh=mesh, in_specs=(row_spec, row_spec, expert_spec, expert_spec), out_specs=row_spec, check_vma=False)

time: 157 us -> 143 us (0.911)
  Pallas kernels: 151 us -> 139 us
  local copies, waits for them, and re-layouts: 5 us -> 2.07 us
    pallas_call x1, Pallas kernels: 151 us -> 139 us  [local_step(): pl.pallas_call(functools.partial(moe_kernel, n_ep, n_dp, capacity, src_ca...]
    unnamed x6 -> x5, local copies, waits for them, and re-layouts: 3.81 us -> 2.07 us
where the time goes in v3:
time: 143 us; the launch traced here: 142 us
  Pallas kernels  139 us (97%)
  local copies, waits for them, and re-layouts  2.07 us (1%)
    pallas_call x1, Pallas kernels, local_step(): pl.pallas_call(functools.partial(moe_kernel, n_ep, n_dp, capacity, src_ca...  139 us

profile of v3, /device:TPU:21, one launch (start us, length us, event | category | flops | bytes accessed | tf_op | source)
XLA Modules:
  0.0 142.4 jit_solution(3576868511577293657)
XLA Ops:
  0.0 0.0 copy-start
  0.0 0.0 copy-start.5
  0.0 139.4 %moe_layer.1 = (bf16[512,768]{1,0:T(8,128)(2,1)}, f32[1]{0:T(128)}) custom-call(bf16[512,768]{1,0:T(8,128)(2,1)} %x_ref.1, f32[64,512]{1,0:T(8,128)} %bitcast.105, bf16[4,768,3072]{2,1,0:T(8,128)(2,1)} %w1_hbm.1, bf16[4,3072,768]{2,1,0:T(8,128)(2,1)} %w2_hbm.1), custom_call_target="tpu_custom_call" | custom-call | tf_op jit(solution)/shard_map/moe_layer/pallas_call | solution.py:404
  140.1 0.0 copy-done
  140.1 0.0 copy-done.5
  140.1 0.2 conditional.1
  140.3 2.1 %copy.47 = bf16[512,768]{1,0:T(8,128)(2,1)} copy(bf16[512,768]{1,0:T(8,128)(2,1)} %get-tuple-element.29) | data formatting | bytes 1572864
Async XLA Ops:
  0.0 140.1 %copy-start = (bf16[512,768]{1,0:T(8,128)(2,1)S(1)}, bf16[512,768]{1,0:T(8,128)(2,1)}, u32[]{:S(2)}) copy-start(bf16[512,768]{1,0:T(8,128)(2,1)} %x_ref.1) | copy-start | bytes 2359300
  0.0 140.1 %copy-start.5 = (f32[512,64]{0,1:T(8,128)S(1)}, f32[512,64]{0,1:T(8,128)}, u32[]{:S(2)}) copy-start(f32[512,64]{0,1:T(8,128)} %param.7) | copy-start | bytes 393220

commit v4 on v3

--- a/solution.py
+++ b/solution.py
@@ -37,7 +37,7 @@
 
 def moe_kernel(n_ep, n_dp, capacity, src_cap, x_ref, lg_ref, w1_hbm, w2_hbm, out_ref, flag_ref,
                w1_buf, w2_buf, blk, near, hops_a, hops_b, hops_c, hops_d, key_send, key_near, key_ring, key_mir,
-               count_send, count_all, acc, z_acc, skey, rkeys, ret, back, y_acc, flag_buf,
+               count_send, count_all, acc, z_acc, skey, rkeys, ret, back, flag_buf,
                w_sem, send_sem, recv_sem, mir_send, mir_recv, px_sem, ksend_sem, krecv_sem, kmir_send, kmir_recv,
                kpx_sem, count_ssem, count_rsem, ret_ssem, ret_rsem, flag_ssem, flag_rsem):
     tok, d_model = x_ref.shape
@@ -76,12 +76,8 @@
     row_i = lax.broadcasted_iota(jnp.int32, (tok, tok), 0)
     col_i = lax.broadcasted_iota(jnp.int32, (tok, tok), 1)
     upper = as_one(row_i < col_i).astype(BF)
-    rank_t = dot(as_one(first_t | second_t).astype(BF), upper)
     e_ids = iota_f((experts, tok), 0)
-    ranks, ids = [], []
-    for mask in (first_t, second_t):
-        ids.append(jnp.sum(jnp.where(mask, e_ids, 0.0), axis=0, keepdims=True))
-        ranks.append(jnp.sum(jnp.where(mask, rank_t, 0.0), axis=0, keepdims=True))
+    ids = [jnp.sum(jnp.where(mask, e_ids, 0.0), axis=0, keepdims=True) for mask in (first_t, second_t)]
     chip_f = chip.astype(F32)
     base = me.astype(F32) * float(experts * src_cap)
     reach = [jnp.zeros((1, tok), F32), jnp.zeros((1, tok), F32)]
@@ -98,10 +94,8 @@
              jnp.where(opposite & jnp.logical_not(forward), float(half), reach[1])]
 
     zero_row = jnp.zeros((1, tok), F32)
-    info = jnp.concatenate([ids[0], ranks[0], ids[1], ranks[1], zero_row + 1.0, zero_row, zero_row, zero_row], axis=0).astype(BF)
     over = jnp.zeros((1, 1), F32)
-    x_val = x_ref[...]
-    near[0:tok, :] = x_val
+    places = []
     for way in range(2):
         level = float(half) - iota_f((8, tok), 0)
         member = as_one((reach[way] == level) & (level > 0.5))
@@ -113,14 +107,77 @@
             place = jnp.where(member[lev:lev + 1] > 0.5, inner[lev:lev + 1] + total, place)
             total = total + sizes[lev:lev + 1]
             over = jnp.maximum(over, as_one(total > float(bounds[lev + 1])))
-        pick = as_one(iota_f((HOP_ROWS[0], tok), 0) == place).astype(BF)
-        blk[way] = dot(pick, x_val).astype(BF)
-        keys = lax.dot_general(info, pick, (((1,), (1,)), ((), ())), preferred_element_type=F32)
+        places.append(place)
+
+    x_val = x_ref[...]
+
+    def pick_rows(way, lo, size):
+        return as_one(iota_f((size, tok), 0) + float(lo) == places[way]).astype(BF)
+
+    def pack_rows(way, lo, size):
+        blk[way, lo:lo + size, :] = dot(pick_rows(way, lo, size), x_val).astype(BF)
+
+    for way in range(2):
+        pack_rows(way, 0, bounds[1])
+
+    def remote(src, dst, send, recv, to):
+        return pltpu.make_async_remote_copy(
+            src_ref=src, dst_ref=dst, send_sem=send, recv_sem=recv, device_id=to, device_id_type=MESH)
+
+    def count_copy(step):
+        return remote(count_send, count_all.at[me], count_ssem.at[step], count_rsem.at[step],
+                      {'ep': lax.rem(me + step, n_ep)})
+
+    def ring_rows(way, hop, lo, size):
+        return hop_bufs[hop].at[pl.ds(way * HOP_ROWS[hop] + lo, size)]
+
+    def hop_copy(way, hop, part):
+        lo, size = bounds[part], bounds[part + 1] - bounds[part]
+        src = blk.at[way, pl.ds(lo, size)] if hop == 0 else ring_rows(way, hop - 1, lo, size)
+        return remote(src, ring_rows(way, hop, lo, size), send_sem.at[way, hop, part], recv_sem.at[way, hop, part],
+                      {'ep': nxt[way]})
+
+    def key_copy(way, hop):
+        src = key_send.at[way] if hop == 0 else key_ring.at[way, hop - 1]
+        return remote(src, key_ring.at[way, hop], ksend_sem.at[way, hop], krecv_sem.at[way, hop], {'ep': nxt[way]})
+
+    def mirror_copy(way, hop):
+        return remote(ring_rows(way, hop, 0, HOP_ROWS[hop]), ring_rows(2 + way, hop, 0, HOP_ROWS[hop]),
+                      mir_send.at[way, hop], mir_recv.at[way, hop], {'ep': other})
+
+    def key_mirror(way, hop):
+        return remote(key_ring.at[way, hop], key_mir.at[way, hop], kmir_send.at[way, hop], kmir_recv.at[way, hop],
+                      {'ep': other})
+
+    px_copy = remote(x_ref, near.at[pl.ds(tok, tok)], px_sem.at[0], px_sem.at[1], {'ep': other})
+    kpx_copy = remote(key_near.at[0], key_near.at[1], kpx_sem.at[0], kpx_sem.at[1], {'ep': other})
+
+    def parts_of(hop):
+        return [p for p in range(half - hop) if bounds[p + 1] > bounds[p]]
+
+    pl.semaphore_wait(barrier, n_ep - 1 + n_dp - 1)
+    for way in range(2):
+        hop_copy(way, 0, 0).start()
+    px_copy.start()
+
+    rank_t = dot(as_one(first_t | second_t).astype(BF), upper)
+    ranks = [jnp.sum(jnp.where(mask, rank_t, 0.0), axis=0, keepdims=True) for mask in (first_t, second_t)]
+    info = jnp.concatenate([ids[0], ranks[0], ids[1], ranks[1], zero_row + 1.0, zero_row, zero_row, zero_row], axis=0).astype(BF)
+    for way in range(2):
+        keys = lax.dot_general(info, pick_rows(way, 0, HOP_ROWS[0]), (((1,), (1,)), ((), ())), preferred_element_type=F32)
         for c in range(2):
             key = base + keys[2 * c:2 * c + 1] * float(src_cap) + keys[2 * c + 1:2 * c + 2]
             key_send[way, c:c + 1, 0:HOP_ROWS[0]] = jnp.where(keys[4:5] > 0.5, key, -1.0)
     for c in range(2):
         key_near[0, c:c + 1, :] = base + ids[c] * float(src_cap) + ranks[c]
+    near[0:tok, :] = x_val
+    for way in range(2):
+        pack_rows(way, bounds[1], HOP_ROWS[0] - bounds[1])
+    for way in range(2):
+        key_copy(way, 0).start()
+        for part in parts_of(0)[1:]:
+            hop_copy(way, 0, part).start()
+    kpx_copy.start()
 
     best, runner, first, second = top_two(logits, 1)
     chosen = as_one(first | second)
@@ -134,53 +191,8 @@
     gates = (1.0 / norm, jnp.exp(runner - best) / norm)
     tkeys = [jnp.sum(jnp.where(mask, lane_e * float(src_cap) + rank, 0.0), axis=1, keepdims=True) for mask in (first, second)]
 
-    pl.semaphore_wait(barrier, n_ep - 1 + n_dp - 1)
-
-    def remote(src, dst, send, recv, to):
-        return pltpu.make_async_remote_copy(
-            src_ref=src, dst_ref=dst, send_sem=send, recv_sem=recv, device_id=to, device_id_type=MESH)
-
-    def count_copy(step):
-        return remote(count_send, count_all.at[me], count_ssem.at[step], count_rsem.at[step],
-                      {'ep': lax.rem(me + step, n_ep)})
-
-    def ring_rows(way, hop, lo, size):
-        return hop_bufs[hop].at[pl.ds(way * HOP_ROWS[hop] + lo, size)]
-
-    def hop_copy(way, hop, part):
-        lo, size = bounds[part], bounds[part + 1] - bounds[part]
-        src = blk.at[way, pl.ds(lo, size)] if hop == 0 else ring_rows(way, hop - 1, lo, size)
-        return remote(src, ring_rows(way, hop, lo, size), send_sem.at[way, hop, part], recv_sem.at[way, hop, part],
-                      {'ep': nxt[way]})
-
-    def key_copy(way, hop):
-        src = key_send.at[way] if hop == 0 else key_ring.at[way, hop - 1]
-        return remote(src, key_ring.at[way, hop], ksend_sem.at[way, hop], krecv_sem.at[way, hop], {'ep': nxt[way]})
-
-    def mirror_copy(way, hop):
-        return remote(ring_rows(way, hop, 0, HOP_ROWS[hop]), ring_rows(2 + way, hop, 0, HOP_ROWS[hop]),
-                      mir_send.at[way, hop], mir_recv.at[way, hop], {'ep': other})
-
-    def key_mirror(way, hop):
-        return remote(key_ring.at[way, hop], key_mir.at[way, hop], kmir_send.at[way, hop], kmir_recv.at[way, hop],
-                      {'ep': other})
-
-    px_copy = remote(x_ref, near.at[pl.ds(tok, tok)], px_sem.at[0], px_sem.at[1], {'ep': other})
-    kpx_copy = remote(key_near.at[0], key_near.at[1], kpx_sem.at[0], kpx_sem.at[1], {'ep': other})
-
-    def parts_of(hop):
-        return [p for p in range(half - hop) if bounds[p + 1] > bounds[p]]
-
-    for way in range(2):
-        hop_copy(way, 0, 0).start()
     for step in range(1, n_ep):
         count_copy(step).start()
-    px_copy.start()
-    kpx_copy.start()
-    for way in range(2):
-        key_copy(way, 0).start()
-        for part in parts_of(0)[1:]:
-            hop_copy(way, 0, part).start()
 
     for step in range(1, n_ep):
         count_copy(step).wait_recv()
@@ -210,11 +222,11 @@
         part = dot(hit, buf[...])
         return part if first_time else acc[el] + part
 
-    def gather_all(buf, keys, first_time=False):
+    def gather_some(lo, hi, buf, keys, first_time=False):
         def body(el, carry):
             acc[el] = gather_rows(el, buf, keys, first_time)
             return carry
-        lax.fori_loop(0, exp_dev, body, 0)
+        lax.fori_loop(lo, hi, body, 0)
 
     def hop_keys(hop):
         for way in range(2):
@@ -225,10 +237,14 @@
 
     px_copy.wait_recv()
     kpx_copy.wait_recv()
-    gather_all(near, jnp.concatenate([key_near[0], key_near[1]], axis=1), True)
-
+    gather_some(0, exp_dev, near, jnp.concatenate([key_near[0], key_near[1]], axis=1), True)
+
+    late = None
     for hop in range(half):
         for part in parts_of(hop):
+            if part == 1 and late is not None:
+                gather_some(exp_dev // 2, exp_dev, *late)
+                late = None
             for way in range(2):
                 hop_copy(way, hop, part).wait_recv()
                 onward = hop + 1 < half
@@ -241,8 +257,15 @@
                         key_copy(way, hop + 1).start()
         for way in range(2):
             mirror_copy(way, hop).start()
+        if late is not None:
+            gather_some(exp_dev // 2, exp_dev, *late)
+            late = None
         if hop + 1 < half:
-            gather_all(hop_bufs[hop], hop_keys(hop))
+            late = (hop_bufs[hop], hop_keys(hop))
+            gather_some(0, exp_dev // 2, *late)
+            if hop + 2 == half:
+                gather_some(exp_dev // 2, exp_dev, *late)
+                late = None
     last_keys = hop_keys(half - 1)
 
     flag_buf[0] = jnp.broadcast_to(over, (8, 128))
@@ -297,7 +320,7 @@
 
     slot_i = lax.broadcasted_iota(jnp.int32, (1, n_ep * src_cap), 1)
     slot_src = lax.div(slot_i, src_cap)
-    y_acc[...] = jnp.zeros_like(y_acc)
+    out_ref[...] = jnp.zeros_like(out_ref)
 
     def mix_body(el, carry):
         for step in ret_order:
@@ -305,11 +328,10 @@
         slot_key = ((slot_src * exp_dev + el) * src_cap + (slot_i - slot_src * src_cap)).astype(F32)
         for c in range(2):
             hit = as_one(tkeys[c] == slot_key).astype(BF)
-            y_acc[...] += gates[c] * dot(hit, back[el])
+            out_ref[...] += gates[c] * dot(hit, back[el])
         return carry
 
     lax.fori_loop(0, exp_dev, mix_body, 0)
-    out_ref[...] = (x_ref[...].astype(F32) + y_acc[...]).astype(BF)
 
     worst = flag_buf[0]
     for step in range(1, n_dp):
@@ -380,8 +402,7 @@
 
     rows_back = jnp.take(ret_buf, send_row, axis=0, mode='fill', fill_value=0)
     pick_gate = jnp.take_along_axis(gate_probs, top_ids, axis=1)
-    mix_sum = jnp.sum(pick_gate[:, :, None] * rows_back.astype(jnp.float32), axis=1)
-    return (x_rows.astype(jnp.float32) + mix_sum).astype(jnp.bfloat16)
+    return jnp.sum(pick_gate[:, :, None] * rows_back.astype(jnp.float32), axis=1)
 
 
 def solution(mesh):
@@ -403,7 +424,7 @@
         dma = pltpu.SemaphoreType.DMA
         out, flag = pl.pallas_call(
             functools.partial(moe_kernel, n_ep, n_dp, capacity, src_cap),
-            out_shape=(jax.ShapeDtypeStruct((tok, d_model), BF), jax.ShapeDtypeStruct((1,), F32)),
+            out_shape=(jax.ShapeDtypeStruct((tok, d_model), F32), jax.ShapeDtypeStruct((1,), F32)),
             in_specs=[vmem, vmem, hbm, hbm],
             out_specs=(vmem, smem),
             scratch_shapes=[
@@ -424,7 +445,6 @@
                 pltpu.VMEM((8, capacity), F32),
                 pltpu.VMEM((exp_dev, n_ep * src_cap, d_model), BF),
                 pltpu.VMEM((exp_dev, n_ep * src_cap, d_model), BF),
-                pltpu.VMEM((tok, d_model), F32),
                 pltpu.VMEM((n_dp, 8, 128), F32),
                 dma((2, 2)),
                 dma((2, half, half)), dma((2, half, half)),
@@ -440,6 +460,7 @@
                 collective_id=0, has_side_effects=True, vmem_limit_bytes=62 * 1024 * 1024),
             name='moe_layer',
         )(x_rows, logits.T, w_in, w_out)
-        return lax.cond(flag[0] > 0.0, functools.partial(plain_step, n_ep), lambda *_: out, x_rows, logits, w_in, w_out)
+        mix_sum = lax.cond(flag[0] > 0.0, functools.partial(plain_step, n_ep), lambda *_: out, x_rows, logits, w_in, w_out)
+        return (x_rows.astype(F32) + mix_sum).astype(BF)
 
     return jax.shard_map(local_step, mesh=mesh, in_specs=(row_spec, row_spec, expert_spec, expert_spec), out_specs=row_spec, check_vma=False)

time: 143 us -> 150 us (1.049)
  Pallas kernels: 139 us -> 146 us
  other arithmetic: 0 us -> 2.44 us
  local copies, waits for them, and re-layouts: 2.07 us -> 0.01 us
    pallas_call x1, Pallas kernels: 139 us -> 146 us  [local_step(): pl.pallas_call(functools.partial(moe_kernel, n_ep, n_dp, capacity, src_ca...]
    convert_element_type x0 -> x1, other arithmetic: none -> 2.44 us  [local_step(): return (x_rows.astype(F32) + mix_sum).astype(BF)]
    unnamed x5 -> x4, local copies, waits for them, and re-layouts: 2.07 us -> 0.01 us
where the time goes in v4:
time: 150 us; the launch traced here: 149 us
  Pallas kernels  146 us (97%)
  other arithmetic  2.44 us (2%)
    pallas_call x1, Pallas kernels, local_step(): pl.pallas_call(functools.partial(moe_kernel, n_ep, n_dp, capacity, src_ca...  146 us

profile of v4, /device:TPU:21, one launch (start us, length us, event | category | flops | bytes accessed | tf_op | source)
XLA Modules:
  0.0 149.4 jit_solution(1680766214265551716)
XLA Ops:
  0.0 0.0 copy-start
  0.0 0.0 copy-start.3
  0.0 146.0 %moe_layer.1 = (f32[512,768]{1,0:T(8,128)}, f32[1]{0:T(128)}) custom-call(bf16[512,768]{1,0:T(8,128)(2,1)} %x_ref.1, f32[64,512]{1,0:T(8,128)} %bitcast.105, bf16[4,768,3072]{2,1,0:T(8,128)(2,1)} %w1_hbm.1, bf16[4,3072,768]{2,1,0:T(8,128)(2,1)} %w2_hbm.1), custom_call_target="tpu_custom_call" | custom-call | tf_op jit(solution)/shard_map/moe_layer/pallas_call | solution.py:425
  146.7 0.0 copy-done
  146.7 0.0 copy-done.3
  146.7 0.3 conditional.1
  146.9 2.4 %add_convert_fusion = bf16[512,768]{1,0:T(8,128)(2,1)} fusion(f32[512,768]{1,0:T(8,128)} %get-tuple-element.114, bf16[512,768]{1,0:T(8,128)(2,1)S(1)} %copy-done), kind=kLoop, calls=%fused_computation.142 | loop fusion | flops 1179648 | bytes 3145728 | tf_op jit(solution)/shard_map/convert_element_type | solution.py:464
Async XLA Ops:
  0.0 146.7 %copy-start = (bf16[512,768]{1,0:T(8,128)(2,1)S(1)}, bf16[512,768]{1,0:T(8,128)(2,1)}, u32[]{:S(2)}) copy-start(bf16[512,768]{1,0:T(8,128)(2,1)} %x_ref.1) | copy-start | bytes 2359300
  0.0 146.7 %copy-start.3 = (f32[512,64]{0,1:T(8,128)S(1)}, f32[512,64]{0,1:T(8,128)}, u32[]{:S(2)}) copy-start(f32[512,64]{0,1:T(8,128)} %param.7) | copy-start | bytes 393220

commit v5 on v4

--- a/solution.py
+++ b/solution.py
@@ -37,7 +37,7 @@
 
 def moe_kernel(n_ep, n_dp, capacity, src_cap, x_ref, lg_ref, w1_hbm, w2_hbm, out_ref, flag_ref,
                w1_buf, w2_buf, blk, near, hops_a, hops_b, hops_c, hops_d, key_send, key_near, key_ring, key_mir,
-               count_send, count_all, acc, z_acc, skey, rkeys, ret, back, flag_buf,
+               count_send, count_all, acc, z_acc, skey, rkeys, ret, back, y_acc, flag_buf,
                w_sem, send_sem, recv_sem, mir_send, mir_recv, px_sem, ksend_sem, krecv_sem, kmir_send, kmir_recv,
                kpx_sem, count_ssem, count_rsem, ret_ssem, ret_rsem, flag_ssem, flag_rsem):
     tok, d_model = x_ref.shape
@@ -117,6 +117,11 @@
     def pack_rows(way, lo, size):
         blk[way, lo:lo + size, :] = dot(pick_rows(way, lo, size), x_val).astype(BF)
 
+    lanes = 128
+    chosen_t = as_one(first_t | second_t).astype(BF)
+    tally = lax.dot_general(jnp.ones((8, tok), BF), chosen_t, (((1,), (1,)), ((), ())), preferred_element_type=F32)
+    count_send[...] = jnp.concatenate([tally[0:1], jnp.zeros((1, lanes - experts), F32) + over], axis=1)
+    count_all[me] = count_send[...]
     for way in range(2):
         pack_rows(way, 0, bounds[1])
 
@@ -156,43 +161,40 @@
         return [p for p in range(half - hop) if bounds[p + 1] > bounds[p]]
 
     pl.semaphore_wait(barrier, n_ep - 1 + n_dp - 1)
+    for step in range(1, n_ep):
+        count_copy(step).start()
     for way in range(2):
         hop_copy(way, 0, 0).start()
     px_copy.start()
-
-    rank_t = dot(as_one(first_t | second_t).astype(BF), upper)
+    for way in range(2):
+        pack_rows(way, bounds[1], HOP_ROWS[0] - bounds[1])
+    for part in parts_of(0)[1:]:
+        for way in range(2):
+            hop_copy(way, 0, part).start()
+
+    rank_t = dot(chosen_t, upper)
     ranks = [jnp.sum(jnp.where(mask, rank_t, 0.0), axis=0, keepdims=True) for mask in (first_t, second_t)]
     info = jnp.concatenate([ids[0], ranks[0], ids[1], ranks[1], zero_row + 1.0, zero_row, zero_row, zero_row], axis=0).astype(BF)
+    place_cols = jnp.concatenate(places + [zero_row] * 6, axis=0).T
     for way in range(2):
-        keys = lax.dot_general(info, pick_rows(way, 0, HOP_ROWS[0]), (((1,), (1,)), ((), ())), preferred_element_type=F32)
+        pick_t = as_one(iota_f((tok, HOP_ROWS[0]), 1) == place_cols[:, way:way + 1]).astype(BF)
+        keys = dot(info, pick_t)
         for c in range(2):
             key = base + keys[2 * c:2 * c + 1] * float(src_cap) + keys[2 * c + 1:2 * c + 2]
             key_send[way, c:c + 1, 0:HOP_ROWS[0]] = jnp.where(keys[4:5] > 0.5, key, -1.0)
+        key_copy(way, 0).start()
     for c in range(2):
         key_near[0, c:c + 1, :] = base + ids[c] * float(src_cap) + ranks[c]
+    kpx_copy.start()
     near[0:tok, :] = x_val
-    for way in range(2):
-        pack_rows(way, bounds[1], HOP_ROWS[0] - bounds[1])
-    for way in range(2):
-        key_copy(way, 0).start()
-        for part in parts_of(0)[1:]:
-            hop_copy(way, 0, part).start()
-    kpx_copy.start()
 
     best, runner, first, second = top_two(logits, 1)
     chosen = as_one(first | second)
-    lanes = 128
-    count_send[...] = jnp.concatenate(
-        [jnp.sum(chosen, axis=0, keepdims=True), jnp.zeros((1, lanes - experts), F32) + over], axis=1)
-    count_all[me] = count_send[...]
     rank = dot(as_one(row_i > col_i).astype(BF), chosen.astype(BF))
     lane_e = iota_f((tok, experts), 1)
     norm = jnp.sum(jnp.exp(logits - best), axis=1, keepdims=True)
     gates = (1.0 / norm, jnp.exp(runner - best) / norm)
     tkeys = [jnp.sum(jnp.where(mask, lane_e * float(src_cap) + rank, 0.0), axis=1, keepdims=True) for mask in (first, second)]
-
-    for step in range(1, n_ep):
-        count_copy(step).start()
 
     for step in range(1, n_ep):
         count_copy(step).wait_recv()
@@ -320,7 +322,7 @@
 
     slot_i = lax.broadcasted_iota(jnp.int32, (1, n_ep * src_cap), 1)
     slot_src = lax.div(slot_i, src_cap)
-    out_ref[...] = jnp.zeros_like(out_ref)
+    y_acc[...] = jnp.zeros_like(y_acc)
 
     def mix_body(el, carry):
         for step in ret_order:
@@ -328,10 +330,12 @@
         slot_key = ((slot_src * exp_dev + el) * src_cap + (slot_i - slot_src * src_cap)).astype(F32)
         for c in range(2):
             hit = as_one(tkeys[c] == slot_key).astype(BF)
-            out_ref[...] += gates[c] * dot(hit, back[el])
+            y_acc[...] += gates[c] * dot(hit, back[el])
         return carry
 
     lax.fori_loop(0, exp_dev, mix_body, 0)
+
+    out_ref[...] = (x_ref[...].astype(F32) + y_acc[...]).astype(BF)
 
     worst = flag_buf[0]
     for step in range(1, n_dp):
@@ -402,7 +406,8 @@
 
     rows_back = jnp.take(ret_buf, send_row, axis=0, mode='fill', fill_value=0)
     pick_gate = jnp.take_along_axis(gate_probs, top_ids, axis=1)
-    return jnp.sum(pick_gate[:, :, None] * rows_back.astype(jnp.float32), axis=1)
+    mix_sum = jnp.sum(pick_gate[:, :, None] * rows_back.astype(jnp.float32), axis=1)
+    return (x_rows.astype(jnp.float32) + mix_sum).astype(jnp.bfloat16)
 
 
 def solution(mesh):
@@ -424,7 +429,7 @@
         dma = pltpu.SemaphoreType.DMA
         out, flag = pl.pallas_call(
             functools.partial(moe_kernel, n_ep, n_dp, capacity, src_cap),
-            out_shape=(jax.ShapeDtypeStruct((tok, d_model), F32), jax.ShapeDtypeStruct((1,), F32)),
+            out_shape=(jax.ShapeDtypeStruct((tok, d_model), BF), jax.ShapeDtypeStruct((1,), F32)),
             in_specs=[vmem, vmem, hbm, hbm],
             out_specs=(vmem, smem),
             scratch_shapes=[
@@ -445,6 +450,7 @@
                 pltpu.VMEM((8, capacity), F32),
                 pltpu.VMEM((exp_dev, n_ep * src_cap, d_model), BF),
                 pltpu.VMEM((exp_dev, n_ep * src_cap, d_model), BF),
+                pltpu.VMEM((tok, d_model), F32),
                 pltpu.VMEM((n_dp, 8, 128), F32),
                 dma((2, 2)),
                 dma((2, half, half)), dma((2, half, half)),
@@ -460,7 +466,6 @@
                 collective_id=0, has_side_effects=True, vmem_limit_bytes=62 * 1024 * 1024),
             name='moe_layer',
         )(x_rows, logits.T, w_in, w_out)
-        mix_sum = lax.cond(flag[0] > 0.0, functools.partial(plain_step, n_ep), lambda *_: out, x_rows, logits, w_in, w_out)
-        return (x_rows.astype(F32) + mix_sum).astype(BF)
+        return lax.cond(flag[0] > 0.0, functools.partial(plain_step, n_ep), lambda *_: out, x_rows, logits, w_in, w_out)
 
     return jax.shard_map(local_step, mesh=mesh, in_specs=(row_spec, row_spec, expert_spec, expert_spec), out_specs=row_spec, check_vma=False)

time: 150 us -> 145 us (0.967)
  Pallas kernels: 146 us -> 142 us
  other arithmetic: 2.44 us -> 0 us
  local copies, waits for them, and re-layouts: 0.01 us -> 2.07 us
    pallas_call x1, Pallas kernels: 146 us -> 142 us  [local_step(): pl.pallas_call(functools.partial(moe_kernel, n_ep, n_dp, capacity, src_ca...]
    convert_element_type x1 -> x0, other arithmetic: 2.44 us -> none  [local_step(): return (x_rows.astype(F32) + mix_sum).astype(BF)]
    unnamed x4 -> x5, local copies, waits for them, and re-layouts: 0.01 us -> 2.07 us
where the time goes in v5:
time: 145 us
  Pallas kernels  142 us (98%)
  local copies, waits for them, and re-layouts  2.07 us (1%)
    pallas_call x1, Pallas kernels, local_step(): pl.pallas_call(functools.partial(moe_kernel, n_ep, n_dp, capacity, src_ca...  142 us

profile of v5, /device:TPU:21, one launch (start us, length us, event | category | flops | bytes accessed | tf_op | source)
XLA Modules:
  0.0 145.0 jit_solution(2499467713660179872)
XLA Ops:
  0.0 0.0 copy-start
  0.0 0.0 copy-start.5
  0.0 142.0 %moe_layer.1 = (bf16[512,768]{1,0:T(8,128)(2,1)}, f32[1]{0:T(128)}) custom-call(bf16[512,768]{1,0:T(8,128)(2,1)} %x_ref.1, f32[64,512]{1,0:T(8,128)} %bitcast.105, bf16[4,768,3072]{2,1,0:T(8,128)(2,1)} %w1_hbm.1, bf16[4,3072,768]{2,1,0:T(8,128)(2,1)} %w2_hbm.1), custom_call_target="tpu_custom_call" | custom-call | tf_op jit(solution)/shard_map/moe_layer/pallas_call | solution.py:430
  142.7 0.0 copy-done
  142.7 0.0 copy-done.5
  142.7 0.3 conditional.1
  142.9 2.1 %copy.47 = bf16[512,768]{1,0:T(8,128)(2,1)} copy(bf16[512,768]{1,0:T(8,128)(2,1)} %get-tuple-element.29) | data formatting | bytes 1572864
Async XLA Ops:
  0.0 142.7 %copy-start = (bf16[512,768]{1,0:T(8,128)(2,1)S(1)}, bf16[512,768]{1,0:T(8,128)(2,1)}, u32[]{:S(2)}) copy-start(bf16[512,768]{1,0:T(8,128)(2,1)} %x_ref.1) | copy-start | bytes 2359300
  0.0 142.7 %copy-start.5 = (f32[512,64]{0,1:T(8,128)S(1)}, f32[512,64]{0,1:T(8,128)}, u32[]{:S(2)}) copy-start(f32[512,64]{0,1:T(8,128)} %param.7) | copy-start | bytes 393220

commit v6 on v5

--- a/solution.py
+++ b/solution.py
@@ -9,6 +9,7 @@
 
 CAP_FACTOR = 2
 HOP_ROWS = (464, 384, 304, 160)
+RET_ROWS = (272, 192, 128, 64)
 FF_TILE = 512
 BF = jnp.bfloat16
 F32 = jnp.float32
@@ -38,8 +39,10 @@
 def moe_kernel(n_ep, n_dp, capacity, src_cap, x_ref, lg_ref, w1_hbm, w2_hbm, out_ref, flag_ref,
                w1_buf, w2_buf, blk, near, hops_a, hops_b, hops_c, hops_d, key_send, key_near, key_ring, key_mir,
                count_send, count_all, acc, z_acc, skey, rkeys, ret, back, y_acc, flag_buf,
+               z_all, ov_place, ov_blk, ov_a, ov_b, ov_c, ov_d, okey_send, okey_ring, okey_mir,
                w_sem, send_sem, recv_sem, mir_send, mir_recv, px_sem, ksend_sem, krecv_sem, kmir_send, kmir_recv,
-               kpx_sem, count_ssem, count_rsem, ret_ssem, ret_rsem, flag_ssem, flag_rsem):
+               kpx_sem, count_ssem, count_rsem, ret_ssem, ret_rsem, flag_ssem, flag_rsem, z_sem, extra_sem,
+               osend_sem, orecv_sem, omir_sem, okey_sem):
     tok, d_model = x_ref.shape
     experts = lg_ref.shape[0]
     exp_dev = experts // n_ep
@@ -54,6 +57,11 @@
     nxt = (lax.rem(chip + 1, n_chip) * 2 + core, lax.rem(chip + n_chip - 1, n_chip) * 2 + core)
     bounds = (0,) + HOP_ROWS[::-1]
     hop_bufs = (hops_a, hops_b, hops_c, hops_d)
+    ov_bufs = (ov_a, ov_b, ov_c, ov_d)
+    ov_bounds = (0,) + RET_ROWS[::-1]
+    direct = src_cap // 2
+    packed = (n_ep + 2) * direct
+    slots = exp_dev * capacity
 
     def weight_copies(el):
         slot = lax.rem(el, 2)
@@ -166,12 +174,6 @@
     for way in range(2):
         hop_copy(way, 0, 0).start()
     px_copy.start()
-    for way in range(2):
-        pack_rows(way, bounds[1], HOP_ROWS[0] - bounds[1])
-    for part in parts_of(0)[1:]:
-        for way in range(2):
-            hop_copy(way, 0, part).start()
-
     rank_t = dot(chosen_t, upper)
     ranks = [jnp.sum(jnp.where(mask, rank_t, 0.0), axis=0, keepdims=True) for mask in (first_t, second_t)]
     info = jnp.concatenate([ids[0], ranks[0], ids[1], ranks[1], zero_row + 1.0, zero_row, zero_row, zero_row], axis=0).astype(BF)
@@ -187,6 +189,11 @@
         key_near[0, c:c + 1, :] = base + ids[c] * float(src_cap) + ranks[c]
     kpx_copy.start()
     near[0:tok, :] = x_val
+    for way in range(2):
+        pack_rows(way, bounds[1], HOP_ROWS[0] - bounds[1])
+    for part in parts_of(0)[1:]:
+        for way in range(2):
+            hop_copy(way, 0, part).start()
 
     best, runner, first, second = top_two(logits, 1)
     chosen = as_one(first | second)
@@ -216,7 +223,92 @@
         e_base = (me * exp_dev + el).astype(F32) * float(src_cap)
         key = jnp.where(valid, src * float(experts * src_cap) + e_base + rnk, -2.0)
         skey[el] = jnp.broadcast_to(key, (128, capacity)).T
-        rkeys[el:el + 1, :] = jnp.where(valid, src * float(src_cap) + rnk, -1.0)
+        beyond = jnp.where(src == me.astype(F32), 0.0, float(direct)) + float((n_ep - 1) * direct)
+        home = (src == me.astype(F32)) | (src == other.astype(F32))
+        spot = jnp.where(rnk < float(direct), src * float(direct) + rnk, jnp.where(home, beyond + rnk, -1.0))
+        rkeys[el:el + 1, :] = jnp.where(valid, spot, -1.0)
+
+    kept = jnp.clip(float(capacity) - (ends - counts), 0.0, counts)
+    to_chip = as_one(jnp.floor((iota_f((experts, lanes), 0) + 0.5) * (1.0 / (2 * exp_dev))) == iota_f((experts, lanes), 1)).astype(BF)
+    pooled = dot(jnp.maximum(kept - float(direct), 0.0).astype(BF), to_chip)
+
+    def distances(src, origin):
+        dest = jnp.floor((src + 0.5) * 0.5)
+        delta = dest - origin
+        delta = jnp.where(delta < 0.0, delta + n_chip, delta)
+        at_half = delta == float(half)
+        even = src == 2.0 * dest
+        return (jnp.where((delta < half) | (at_half & even), delta, 0.0),
+                jnp.where((delta > half) | (at_half & jnp.logical_not(even)), n_chip - delta, 0.0))
+
+    for dist in distances(iota_f((n_ep, lanes), 0), iota_f((n_ep, lanes), 1)):
+        for hop in range(half):
+            load = jnp.sum(jnp.where(dist >= float(hop + 1), pooled, 0.0), axis=0, keepdims=True)
+            over = jnp.maximum(over, jnp.max(as_one(load > float(2 * RET_ROWS[hop])), axis=1, keepdims=True))
+
+    def plan_overflow():
+        row_c = lax.broadcasted_iota(jnp.int32, (capacity, capacity), 0)
+        col_c = lax.broadcasted_iota(jnp.int32, (capacity, capacity), 1)
+        upper_c = as_one(row_c < col_c).astype(BF)
+        infos, members = [], ([], [])
+        level = float(half) - iota_f((8, capacity), 0)
+        zero_c = jnp.zeros((1, capacity), F32)
+        for b in range(2 * exp_dev):
+            expert_id = chip * 2 * exp_dev + b
+            mine = lane_ep == expert_id
+            count_col = jnp.sum(jnp.where(mine, counts, 0.0), axis=1, keepdims=True)
+            end_col = jnp.sum(jnp.where(mine, ends, 0.0), axis=1, keepdims=True)
+            past = as_one(end_col <= slot)
+            src = jnp.sum(past, axis=0, keepdims=True)
+            rnk = slot[0:1] - jnp.sum(past * count_col, axis=0, keepdims=True)
+            live = (src < float(n_ep)) & (rnk >= float(direct))
+            infos.append(jnp.concatenate([src, zero_c + expert_id.astype(F32), rnk, zero_c + 1.0] + [zero_c] * 4, axis=0).astype(BF))
+            for way, dist in enumerate(distances(src, chip_f)):
+                members[way].append(as_one((jnp.where(live, dist, 0.0) == level) & (level > 0.5)))
+        for way in range(2):
+            inner = dot(jnp.concatenate(members[way], axis=0).astype(BF), upper_c)
+            run = jnp.zeros((8, 1), F32)
+            inners = []
+            for b in range(2 * exp_dev):
+                inners.append(inner[8 * b:8 * b + 8] + run)
+                run = run + jnp.sum(members[way][b], axis=1, keepdims=True)
+            for b in range(2 * exp_dev):
+                place, total = zero_c - 1.0, jnp.zeros((1, 1), F32)
+                for lev in range(half):
+                    place = jnp.where(members[way][b][lev:lev + 1] > 0.5, inners[b][lev:lev + 1] + total, place)
+                    total = total + run[lev:lev + 1]
+                ov_place[way, b:b + 1, :] = place
+            columns = ov_place[way].T
+            keys = jnp.zeros((8, RET_ROWS[0]), F32)
+            turn = 2.0 * iota_f((capacity, RET_ROWS[0]), 1) + core.astype(F32)
+            for b in range(2 * exp_dev):
+                keys = keys + dot(infos[b], as_one(turn == columns[:, b:b + 1]).astype(BF))
+            key = keys[0:1] * float(experts * src_cap) + keys[1:2] * float(src_cap) + keys[2:3]
+            okey_send[way, 0:1, 0:RET_ROWS[0]] = jnp.where(keys[3:4] > 0.5, key, -1.0)
+
+    def ov_rows(way, hop, lo, size):
+        return ov_bufs[hop].at[pl.ds(way * RET_ROWS[hop] + lo, size)]
+
+    def ov_copy(way, hop, part):
+        lo, size = ov_bounds[part], ov_bounds[part + 1] - ov_bounds[part]
+        src = ov_blk.at[way, pl.ds(lo, size)] if hop == 0 else ov_rows(way, hop - 1, lo, size)
+        return remote(src, ov_rows(way, hop, lo, size), osend_sem.at[way, hop, part], orecv_sem.at[way, hop, part],
+                      {'ep': nxt[way]})
+
+    def okey_copy(way, hop):
+        src = okey_send.at[way] if hop == 0 else okey_ring.at[way, hop - 1]
+        return remote(src, okey_ring.at[way, hop], okey_sem.at[way, hop, 0], okey_sem.at[way, hop, 1], {'ep': nxt[way]})
+
+    def ov_mirror(way, hop):
+        return remote(ov_rows(way, hop, 0, RET_ROWS[hop]), ov_rows(2 + way, hop, 0, RET_ROWS[hop]),
+                      omir_sem.at[way, hop, 0], omir_sem.at[way, hop, 1], {'ep': other})
+
+    def okey_mirror(way, hop):
+        return remote(okey_ring.at[way, hop], okey_mir.at[way, hop], okey_sem.at[way, hop, 2], okey_sem.at[way, hop, 3],
+                      {'ep': other})
+
+    def ov_parts(hop):
+        return list(range(half - hop))
 
     def gather_rows(el, buf, keys, first_time=False):
         want = skey[el][:, 0:1]
@@ -224,11 +316,11 @@
         part = dot(hit, buf[...])
         return part if first_time else acc[el] + part
 
-    def gather_some(lo, hi, buf, keys, first_time=False):
+    def gather_all(buf, keys, first_time=False):
         def body(el, carry):
             acc[el] = gather_rows(el, buf, keys, first_time)
             return carry
-        lax.fori_loop(lo, hi, body, 0)
+        lax.fori_loop(0, exp_dev, body, 0)
 
     def hop_keys(hop):
         for way in range(2):
@@ -239,13 +331,15 @@
 
     px_copy.wait_recv()
     kpx_copy.wait_recv()
-    gather_some(0, exp_dev, near, jnp.concatenate([key_near[0], key_near[1]], axis=1), True)
+    gather_all(near, jnp.concatenate([key_near[0], key_near[1]], axis=1), True)
 
     late = None
     for hop in range(half):
         for part in parts_of(hop):
+            if hop == 1 and part == parts_of(1)[-1]:
+                plan_overflow()
             if part == 1 and late is not None:
-                gather_some(exp_dev // 2, exp_dev, *late)
+                gather_all(*late)
                 late = None
             for way in range(2):
                 hop_copy(way, hop, part).wait_recv()
@@ -259,14 +353,10 @@
                         key_copy(way, hop + 1).start()
         for way in range(2):
             mirror_copy(way, hop).start()
-        if late is not None:
-            gather_some(exp_dev // 2, exp_dev, *late)
-            late = None
         if hop + 1 < half:
             late = (hop_bufs[hop], hop_keys(hop))
-            gather_some(0, exp_dev // 2, *late)
             if hop + 2 == half:
-                gather_some(exp_dev // 2, exp_dev, *late)
+                gather_all(*late)
                 late = None
     last_keys = hop_keys(half - 1)
 
@@ -283,10 +373,22 @@
     def ret_copy(el, step):
         dest = lax.rem(me + step, n_ep)
         return pltpu.make_async_remote_copy(
-            src_ref=ret.at[el, pl.ds(pl.multiple_of(dest * src_cap, src_cap), src_cap)],
-            dst_ref=back.at[el, pl.ds(pl.multiple_of(me * src_cap, src_cap), src_cap)],
+            src_ref=ret.at[el, pl.ds(pl.multiple_of(dest * direct, direct), direct)],
+            dst_ref=back.at[el, pl.ds(pl.multiple_of(me * direct, direct), direct)],
             send_sem=ret_ssem.at[el, step], recv_sem=ret_rsem.at[el, step],
             device_id={'ep': dest}, device_id_type=MESH)
+
+    def extra_copy(el):
+        rows = pl.ds(packed - direct, direct)
+        return remote(ret.at[el, rows], back.at[el, rows], extra_sem.at[el, 0], extra_sem.at[el, 1], {'ep': other})
+
+    def z_copy(el):
+        rows = pl.ds(pl.multiple_of(core * slots + el * capacity, capacity), capacity)
+        return remote(z_all.at[rows], z_all.at[rows], z_sem.at[el, 0], z_sem.at[el, 1], {'ep': other})
+
+    def z_arrival(el):
+        rows = pl.ds(pl.multiple_of((1 - core) * slots + el * capacity, capacity), capacity)
+        return remote(z_all.at[rows], z_all.at[rows], z_sem.at[el, 0], z_sem.at[el, 1], {'ep': other})
 
     ret_order = sorted(range(1, n_ep), key=lambda s: -min(s, n_ep - s))
 
@@ -310,24 +412,46 @@
             for copy in weight_copies(el + 2):
                 copy.start()
 
-        spread = as_one(iota_f((n_ep * src_cap, capacity), 0) == rkeys[pl.ds(el, 1), :]).astype(BF)
-        ret[el] = dot(spread, z_acc[...].astype(BF)).astype(BF)
+        spread = as_one(iota_f((packed, capacity), 0) == rkeys[pl.ds(el, 1), :]).astype(BF)
+        z_rows = z_acc[...].astype(BF)
+        z_all[pl.ds(pl.multiple_of(core * slots + el * capacity, capacity), capacity), :] = z_rows
+        ret[el] = dot(spread, z_rows).astype(BF)
         for step in ret_order:
             ret_copy(el, step).start()
-        own = pl.ds(pl.multiple_of(me * src_cap, src_cap), src_cap)
+        extra_copy(el).start()
+        z_copy(el).start()
+        own = pl.ds(pl.multiple_of(me * direct, direct), direct)
         back[el, own, :] = ret[el, own, :]
+        back[el, n_ep * direct:(n_ep + 1) * direct, :] = ret[el, n_ep * direct:(n_ep + 1) * direct, :]
         return carry
 
     lax.fori_loop(0, exp_dev, expert_body, 0)
 
-    slot_i = lax.broadcasted_iota(jnp.int32, (1, n_ep * src_cap), 1)
-    slot_src = lax.div(slot_i, src_cap)
+    for el in range(exp_dev):
+        z_arrival(el).wait_recv()
+    turn = 2.0 * iota_f((RET_ROWS[0], capacity), 0) + core.astype(F32)
+    for way in range(2):
+        take = jnp.concatenate([as_one(turn == ov_place[way, b:b + 1, :]).astype(BF) for b in range(2 * exp_dev)], axis=1)
+        ov_blk[way] = dot(take, z_all[...]).astype(BF)
+    for way in range(2):
+        ov_copy(way, 0, 0).start()
+        okey_copy(way, 0).start()
+    for part in ov_parts(0)[1:]:
+        for way in range(2):
+            ov_copy(way, 0, part).start()
+
+    slot_i = lax.broadcasted_iota(jnp.int32, (1, packed), 1)
+    slot_src = lax.div(slot_i, direct)
+    slot_rank = slot_i - slot_src * direct
+    slot_rank = jnp.where(slot_src < n_ep, slot_rank, slot_rank + direct)
+    slot_src = jnp.where(slot_src < n_ep, slot_src, jnp.where(slot_src == n_ep, me, other))
     y_acc[...] = jnp.zeros_like(y_acc)
 
     def mix_body(el, carry):
         for step in ret_order:
             ret_copy(el, step).wait_recv()
-        slot_key = ((slot_src * exp_dev + el) * src_cap + (slot_i - slot_src * src_cap)).astype(F32)
+        extra_copy(el).wait_recv()
+        slot_key = ((slot_src * exp_dev + el) * src_cap + slot_rank).astype(F32)
         for c in range(2):
             hit = as_one(tkeys[c] == slot_key).astype(BF)
             y_acc[...] += gates[c] * dot(hit, back[el])
@@ -335,6 +459,33 @@
 
     lax.fori_loop(0, exp_dev, mix_body, 0)
 
+    def mix_overflow(hop):
+        for way in range(2):
+            ov_mirror(way, hop).wait_recv()
+            okey_mirror(way, hop).wait_recv()
+        size = RET_ROWS[hop]
+        keys = jnp.concatenate([buf[way, hop][:, 0:size] for buf in (okey_ring, okey_mir) for way in range(2)], axis=1)
+        for c in range(2):
+            hit = as_one(base + tkeys[c] == keys).astype(BF)
+            y_acc[...] += gates[c] * dot(hit, ov_bufs[hop][...])
+
+    for hop in range(half):
+        onward = hop + 1 < half
+        for part in ov_parts(hop):
+            for way in range(2):
+                ov_copy(way, hop, part).wait_recv()
+                if onward and part in ov_parts(hop + 1):
+                    ov_copy(way, hop + 1, part).start()
+                if part == 0:
+                    okey_copy(way, hop).wait_recv()
+                    okey_mirror(way, hop).start()
+                    if onward:
+                        okey_copy(way, hop + 1).start()
+            if part == 0 and hop > 0:
+                mix_overflow(hop - 1)
+        for way in range(2):
+            ov_mirror(way, hop).start()
+    mix_overflow(half - 1)
     out_ref[...] = (x_ref[...].astype(F32) + y_acc[...]).astype(BF)
 
     worst = flag_buf[0]
@@ -357,57 +508,57 @@
             for part in parts_of(hop):
                 hop_copy(way, hop, part).wait_send()
     for el in range(exp_dev):
+        extra_copy(el).wait_send()
+        z_copy(el).wait_send()
         for step in ret_order:
             ret_copy(el, step).wait_send()
+    for hop in range(half):
+        for way in range(2):
+            ov_mirror(way, hop).wait_send()
+            okey_mirror(way, hop).wait_send()
+            okey_copy(way, hop).wait_send()
+            for part in ov_parts(hop):
+                ov_copy(way, hop, part).wait_send()
 
 
 def plain_step(n_ep, x_rows, logits, w_in, w_out):
-    tok_dev, d_model = x_rows.shape
+    tok, d_model = x_rows.shape
     experts = logits.shape[1]
     exp_dev = w_in.shape[0]
-    capacity = CAP_FACTOR * tok_dev * n_ep // experts
-    src_cap = 4 * tok_dev // experts
-    my_index = lax.axis_index('ep')
-    gate_probs = jax.nn.softmax(logits, axis=-1)
-    top_vals, top_ids = lax.top_k(logits, 2)
-    chosen = (logits >= top_vals[:, 1:2]).astype(jnp.int32)
-    local_before = jnp.cumsum(chosen, axis=0) - chosen
-    local_counts = jnp.sum(chosen, axis=0).astype(jnp.float32)
-    all_counts = lax.all_gather(local_counts, 'ep').astype(jnp.int32)
-    dev_offsets = jnp.cumsum(all_counts, axis=0) - all_counts
-    local_pos = jnp.take_along_axis(local_before, top_ids, axis=1)
-    kept_mask = local_pos + jnp.take(dev_offsets[my_index], top_ids) < capacity
-    send_row = jnp.where(kept_mask, top_ids * src_cap + local_pos, experts * src_cap)
-    tok_ids = jnp.broadcast_to(jnp.arange(tok_dev, dtype=jnp.int32)[:, None], (tok_dev, 2))
-    slot_tok = jnp.full((experts * src_cap,), tok_dev, jnp.int32).at[send_row.reshape(-1)].set(tok_ids.reshape(-1), mode='drop')
-    send_buf = jnp.take(x_rows, slot_tok, axis=0, mode='fill', fill_value=0)
+    capacity = CAP_FACTOR * tok * n_ep // experts
+    src_cap = 4 * tok // experts
+    me = lax.axis_index('ep')
+    best, runner, first, second = top_two(logits, 1)
+    norm = jnp.sum(jnp.exp(logits - best), axis=1, keepdims=True)
+    gates = (1.0 / norm, jnp.exp(runner - best) / norm)
+    chosen = as_one(first | second)
+    lower = as_one(iota_f((tok, tok), 0) > iota_f((tok, tok), 1)).astype(BF)
+    rank = dot(lower, chosen.astype(BF))
+    counts = lax.all_gather(jnp.sum(chosen, axis=0), 'ep')
+    tri = as_one(iota_f((n_ep, n_ep), 0) > iota_f((n_ep, n_ep), 1)).astype(BF)
+    before = dot(tri, counts.astype(BF))
+    mine = jnp.sum(jnp.where(iota_f((n_ep, experts), 0) == me.astype(F32), before, 0.0), axis=0, keepdims=True)
+    slot_of = jnp.where(rank + mine < capacity, iota_f((tok, experts), 1) * src_cap + rank, -1.0)
+    rows = [jnp.sum(jnp.where(mask, slot_of, 0.0), axis=1, keepdims=True) for mask in (first, second)]
+    slots = iota_f((tok, experts * src_cap), 1)
+    hits = [as_one(row == slots).astype(BF) for row in rows]
+    send_buf = lax.dot_general(hits[0] + hits[1], x_rows, (((0,), (0,)), ((), ())), preferred_element_type=F32).astype(BF)
     recv_buf = lax.all_to_all(send_buf, 'ep', 0, 0, tiled=True)
-
-    own_counts = lax.dynamic_slice_in_dim(all_counts, my_index * exp_dev, exp_dev, axis=1)
-    own_offsets = lax.dynamic_slice_in_dim(dev_offsets, my_index * exp_dev, exp_dev, axis=1)
-    kept_counts = jnp.minimum(jnp.maximum(capacity - own_offsets, 0), own_counts)
-    slot_ends = (own_offsets + kept_counts).T
-    cap_ids = jnp.arange(capacity, dtype=jnp.int32)
-    below_mask = slot_ends[:, None, :] <= cap_ids[None, :, None]
-    src_dev = jnp.sum(below_mask.astype(jnp.int32), axis=2)
-    slot_start = jnp.sum(jnp.where(below_mask, kept_counts.T[:, None, :], 0), axis=2)
-    exp_local = jnp.arange(exp_dev, dtype=jnp.int32)
-    recv_row = (src_dev * exp_dev + exp_local[:, None]) * src_cap + cap_ids[None, :] - slot_start
-    recv_row = jnp.where(src_dev < n_ep, recv_row, n_ep * exp_dev * src_cap)
-    expert_rows = jnp.take(recv_buf, recv_row.reshape(-1), axis=0, mode='fill', fill_value=0).reshape(exp_dev, capacity, d_model)
-    hidden = jax.nn.gelu(jnp.einsum('ecd,edf->ecf', expert_rows, w_in, preferred_element_type=jnp.float32), approximate=True).astype(jnp.bfloat16)
-    expert_out = jnp.einsum('ecf,efd->ecd', hidden, w_out, preferred_element_type=jnp.float32).astype(jnp.bfloat16).reshape(exp_dev * capacity, d_model)
-
-    src_slots = jnp.arange(src_cap, dtype=jnp.int32)
-    back_row = exp_local[None, :, None] * capacity + own_offsets[:, :, None] + src_slots[None, None, :]
-    back_row = jnp.where(src_slots[None, None, :] < kept_counts[:, :, None], back_row, exp_dev * capacity)
-    back_buf = jnp.take(expert_out, back_row.reshape(-1), axis=0, mode='fill', fill_value=0)
+    own = lax.dynamic_slice_in_dim(jnp.stack([before, counts]), me * exp_dev, exp_dev, axis=2)
+    start = jnp.transpose(own[0])[:, :, None]
+    size = jnp.transpose(own[1])[:, :, None]
+    order = jnp.arange(src_cap, dtype=F32)[None, None, :]
+    place = jnp.where((order < size) & (start + order < capacity), start + order, -1.0)
+    place = jnp.where(place >= 0.0, place + capacity * jnp.arange(exp_dev, dtype=F32)[:, None, None], -1.0)
+    place = jnp.transpose(place, (1, 0, 2)).reshape(1, experts * src_cap)
+    move = as_one(iota_f((exp_dev * capacity, experts * src_cap), 0) == place).astype(BF)
+    expert_rows = dot(move, recv_buf).astype(BF).reshape(exp_dev, capacity, d_model)
+    hidden = jax.nn.gelu(jnp.einsum('ecd,edf->ecf', expert_rows, w_in, preferred_element_type=F32), approximate=True).astype(BF)
+    expert_out = jnp.einsum('ecf,efd->ecd', hidden, w_out, preferred_element_type=F32).astype(BF).reshape(exp_dev * capacity, d_model)
+    back_buf = lax.dot_general(move, expert_out, (((0,), (0,)), ((), ())), preferred_element_type=F32).astype(BF)
     ret_buf = lax.all_to_all(back_buf, 'ep', 0, 0, tiled=True)
-
-    rows_back = jnp.take(ret_buf, send_row, axis=0, mode='fill', fill_value=0)
-    pick_gate = jnp.take_along_axis(gate_probs, top_ids, axis=1)
-    mix_sum = jnp.sum(pick_gate[:, :, None] * rows_back.astype(jnp.float32), axis=1)
-    return (x_rows.astype(jnp.float32) + mix_sum).astype(jnp.bfloat16)
+    mix_sum = gates[0] * dot(hits[0], ret_buf) + gates[1] * dot(hits[1], ret_buf)
+    return (x_rows.astype(F32) + mix_sum).astype(BF)
 
 
 def solution(mesh):
@@ -423,6 +574,7 @@
         capacity = CAP_FACTOR * tok * n_ep // experts
         src_cap = 4 * tok // experts
         half = n_ep // 4
+        packed = (n_ep + 2) * (src_cap // 2)
         vmem = pl.BlockSpec(memory_space=pltpu.VMEM)
         smem = pl.BlockSpec(memory_space=pltpu.SMEM)
         hbm = pl.BlockSpec(memory_space=pl.ANY)
@@ -448,10 +600,17 @@
                 pltpu.VMEM((capacity, d_model), F32),
                 pltpu.VMEM((exp_dev, capacity, 128), F32),
                 pltpu.VMEM((8, capacity), F32),
-                pltpu.VMEM((exp_dev, n_ep * src_cap, d_model), BF),
-                pltpu.VMEM((exp_dev, n_ep * src_cap, d_model), BF),
+                pltpu.VMEM((exp_dev, packed, d_model), BF),
+                pltpu.VMEM((exp_dev, packed, d_model), BF),
                 pltpu.VMEM((tok, d_model), F32),
                 pltpu.VMEM((n_dp, 8, 128), F32),
+                pltpu.VMEM((2 * exp_dev * capacity, d_model), BF),
+                pltpu.VMEM((2, 2 * exp_dev, capacity), F32),
+                pltpu.VMEM((2, RET_ROWS[0], d_model), BF),
+                *[pltpu.VMEM((4 * rows, d_model), BF) for rows in RET_ROWS],
+                pltpu.VMEM((2, 1, tok), F32),
+                pltpu.VMEM((2, half, 1, tok), F32),
+                pltpu.VMEM((2, half, 1, tok), F32),
                 dma((2, 2)),
                 dma((2, half, half)), dma((2, half, half)),
                 dma((2, half)), dma((2, half)),
@@ -461,6 +620,9 @@
                 dma((n_ep,)), dma((n_ep,)),
                 dma((exp_dev, n_ep)), dma((exp_dev, n_ep)),
                 dma((n_dp,)), dma((n_dp,)),
+                dma((exp_dev, 2)), dma((exp_dev, 2)),
+                dma((2, half, half)), dma((2, half, half)),
+                dma((2, half, 2)), dma((2, half, 4)),
             ],
             compiler_params=pltpu.CompilerParams(
                 collective_id=0, has_side_effects=True, vmem_limit_bytes=62 * 1024 * 1024),

time: 145 us -> 133 us (0.917)
  Pallas kernels: 142 us -> 130 us
    pallas_call x1, Pallas kernels: 142 us -> 130 us  [local_step(): pl.pallas_call(functools.partial(moe_kernel, n_ep, n_dp, capacity, src_ca...]
where the time goes in v6:
time: 133 us
  Pallas kernels  130 us (98%)
  local copies, waits for them, and re-layouts  2.07 us (2%)
    pallas_call x1, Pallas kernels, local_step(): pl.pallas_call(functools.partial(moe_kernel, n_ep, n_dp, capacity, src_ca...  130 us

profile of v6, /device:TPU:21, one launch (start us, length us, event | category | flops | bytes accessed | tf_op | source)
XLA Modules:
  0.0 132.7 jit_solution(737245186778086808)
XLA Ops:
  0.0 0.0 copy-start
  0.0 0.0 copy-start.1
  0.0 129.8 %moe_layer.1 = (bf16[512,768]{1,0:T(8,128)(2,1)}, f32[1]{0:T(128)}) custom-call(bf16[512,768]{1,0:T(8,128)(2,1)} %x_ref.1, f32[64,512]{1,0:T(8,128)} %bitcast.28, bf16[4,768,3072]{2,1,0:T(8,128)(2,1)} %w1_hbm.1, bf16[4,3072,768]{2,1,0:T(8,128)(2,1)} %w2_hbm.1), custom_call_target="tpu_custom_call" | custom-call | tf_op jit(solution)/shard_map/moe_layer/pallas_call | solution.py:582
  130.6 0.0 copy-done
  130.6 0.0 copy-done.1
  130.6 2.1 %copy.24 = bf16[512,768]{1,0:T(8,128)(2,1)} copy(bf16[512,768]{1,0:T(8,128)(2,1)} %get-tuple-element.25) | data formatting | bytes 1572864
  (1 shorter events, 0.0 us)
Async XLA Ops:
  0.0 130.6 %copy-start = (f32[512,64]{0,1:T(8,128)S(1)}, f32[512,64]{0,1:T(8,128)}, u32[]{:S(2)}) copy-start(f32[512,64]{0,1:T(8,128)} %param.7) | copy-start | bytes 393220
  0.0 130.6 %copy-start.1 = (bf16[512,768]{1,0:T(8,128)(2,1)S(1)}, bf16[512,768]{1,0:T(8,128)(2,1)}, u32[]{:S(2)}) copy-start(bf16[512,768]{1,0:T(8,128)(2,1)} %x_ref.1) | copy-start | bytes 2359300

commit v7 on v6

--- a/solution.py
+++ b/solution.py
@@ -9,7 +9,8 @@
 
 CAP_FACTOR = 2
 HOP_ROWS = (464, 384, 304, 160)
-RET_ROWS = (272, 192, 128, 64)
+RET_ROWS = (416, 320, 208, 80)
+DIRECT_PART = 4
 FF_TILE = 512
 BF = jnp.bfloat16
 F32 = jnp.float32
@@ -59,8 +60,9 @@
     hop_bufs = (hops_a, hops_b, hops_c, hops_d)
     ov_bufs = (ov_a, ov_b, ov_c, ov_d)
     ov_bounds = (0,) + RET_ROWS[::-1]
-    direct = src_cap // 2
-    packed = (n_ep + 2) * direct
+    direct = src_cap // DIRECT_PART
+    extra = src_cap - direct
+    packed = n_ep * direct + 2 * extra
     slots = exp_dev * capacity
 
     def weight_copies(el):
@@ -223,7 +225,7 @@
         e_base = (me * exp_dev + el).astype(F32) * float(src_cap)
         key = jnp.where(valid, src * float(experts * src_cap) + e_base + rnk, -2.0)
         skey[el] = jnp.broadcast_to(key, (128, capacity)).T
-        beyond = jnp.where(src == me.astype(F32), 0.0, float(direct)) + float((n_ep - 1) * direct)
+        beyond = jnp.where(src == me.astype(F32), 0.0, float(extra)) + float((n_ep - 1) * direct)
         home = (src == me.astype(F32)) | (src == other.astype(F32))
         spot = jnp.where(rnk < float(direct), src * float(direct) + rnk, jnp.where(home, beyond + rnk, -1.0))
         rkeys[el:el + 1, :] = jnp.where(valid, spot, -1.0)
@@ -379,7 +381,7 @@
             device_id={'ep': dest}, device_id_type=MESH)
 
     def extra_copy(el):
-        rows = pl.ds(packed - direct, direct)
+        rows = pl.ds(packed - extra, extra)
         return remote(ret.at[el, rows], back.at[el, rows], extra_sem.at[el, 0], extra_sem.at[el, 1], {'ep': other})
 
     def z_copy(el):
@@ -422,7 +424,7 @@
         z_copy(el).start()
         own = pl.ds(pl.multiple_of(me * direct, direct), direct)
         back[el, own, :] = ret[el, own, :]
-        back[el, n_ep * direct:(n_ep + 1) * direct, :] = ret[el, n_ep * direct:(n_ep + 1) * direct, :]
+        back[el, packed - 2 * extra:packed - extra, :] = ret[el, packed - 2 * extra:packed - extra, :]
         return carry
 
     lax.fori_loop(0, exp_dev, expert_body, 0)
@@ -443,8 +445,10 @@
     slot_i = lax.broadcasted_iota(jnp.int32, (1, packed), 1)
     slot_src = lax.div(slot_i, direct)
     slot_rank = slot_i - slot_src * direct
-    slot_rank = jnp.where(slot_src < n_ep, slot_rank, slot_rank + direct)
-    slot_src = jnp.where(slot_src < n_ep, slot_src, jnp.where(slot_src == n_ep, me, other))
+    past_own = slot_i - n_ep * direct
+    past_other = past_own - extra
+    slot_src = jnp.where(past_own < 0, slot_src, jnp.where(past_other < 0, me, other))
+    slot_rank = jnp.where(past_own < 0, slot_rank, jnp.where(past_other < 0, past_own, past_other) + direct)
     y_acc[...] = jnp.zeros_like(y_acc)
 
     def mix_body(el, carry):
@@ -481,10 +485,12 @@
                     okey_mirror(way, hop).start()
                     if onward:
                         okey_copy(way, hop + 1).start()
-            if part == 0 and hop > 0:
+            if part == 0 and hop > 0 and onward:
                 mix_overflow(hop - 1)
         for way in range(2):
             ov_mirror(way, hop).start()
+        if not onward:
+            mix_overflow(hop - 1)
     mix_overflow(half - 1)
     out_ref[...] = (x_ref[...].astype(F32) + y_acc[...]).astype(BF)
 
@@ -574,7 +580,7 @@
         capacity = CAP_FACTOR * tok * n_ep // experts
         src_cap = 4 * tok // experts
         half = n_ep // 4
-        packed = (n_ep + 2) * (src_cap // 2)
+        packed = n_ep * (src_cap // DIRECT_PART) + 2 * (src_cap - src_cap // DIRECT_PART)
         vmem = pl.BlockSpec(memory_space=pltpu.VMEM)
         smem = pl.BlockSpec(memory_space=pltpu.SMEM)
         hbm = pl.BlockSpec(memory_space=pl.ANY)

time: 133 us -> 133 us (level)
  no operation moved by 1% of the time
where the time goes in v7:
time: 133 us
  Pallas kernels  130 us (98%)
  local copies, waits for them, and re-layouts  2.07 us (2%)
    pallas_call x1, Pallas kernels, local_step(): pl.pallas_call(functools.partial(moe_kernel, n_ep, n_dp, capacity, src_ca...  130 us

profile of v7, /device:TPU:21, one launch (start us, length us, event | category | flops | bytes accessed | tf_op | source)
XLA Modules:
  0.0 132.8 jit_solution(10299775091263651963)
XLA Ops:
  0.0 0.0 copy-start
  0.0 0.0 copy-start.1
  0.0 130.0 %moe_layer.1 = (bf16[512,768]{1,0:T(8,128)(2,1)}, f32[1]{0:T(128)}) custom-call(bf16[512,768]{1,0:T(8,128)(2,1)} %x_ref.1, f32[64,512]{1,0:T(8,128)} %bitcast.28, bf16[4,768,3072]{2,1,0:T(8,128)(2,1)} %w1_hbm.1, bf16[4,3072,768]{2,1,0:T(8,128)(2,1)} %w2_hbm.1), custom_call_target="tpu_custom_call" | custom-call | tf_op jit(solution)/shard_map/moe_layer/pallas_call | solution.py:588
  130.7 0.0 copy-done
  130.7 0.0 copy-done.1
  130.7 2.1 %copy.24 = bf16[512,768]{1,0:T(8,128)(2,1)} copy(bf16[512,768]{1,0:T(8,128)(2,1)} %get-tuple-element.25) | data formatting | bytes 1572864
  (1 shorter events, 0.0 us)
Async XLA Ops:
  0.0 130.7 %copy-start = (f32[512,64]{0,1:T(8,128)S(1)}, f32[512,64]{0,1:T(8,128)}, u32[]{:S(2)}) copy-start(f32[512,64]{0,1:T(8,128)} %param.7) | copy-start | bytes 393220
  0.0 130.7 %copy-start.1 = (bf16[512,768]{1,0:T(8,128)(2,1)S(1)}, bf16[512,768]{1,0:T(8,128)(2,1)}, u32[]{:S(2)}) copy-start(bf16[512,768]{1,0:T(8,128)(2,1)} %x_ref.1) | copy-start | bytes 2359300

commit v8 on v6

--- a/solution.py
+++ b/solution.py
@@ -331,9 +331,8 @@
 
     px_copy.wait_recv()
     kpx_copy.wait_recv()
-    gather_all(near, jnp.concatenate([key_near[0], key_near[1]], axis=1), True)
-
-    late = None
+
+    late = (near, jnp.concatenate([key_near[0], key_near[1]], axis=1), True)
     for hop in range(half):
         for part in parts_of(hop):
             if hop == 1 and part == parts_of(1)[-1]:
@@ -481,10 +480,12 @@
                     okey_mirror(way, hop).start()
                     if onward:
                         okey_copy(way, hop + 1).start()
-            if part == 0 and hop > 0:
+            if part == 0 and hop > 0 and onward:
                 mix_overflow(hop - 1)
         for way in range(2):
             ov_mirror(way, hop).start()
+        if not onward:
+            mix_overflow(hop - 1)
     mix_overflow(half - 1)
     out_ref[...] = (x_ref[...].astype(F32) + y_acc[...]).astype(BF)
 

time: 133 us -> 132 us (level)
  no operation moved by 1% of the time
where the time goes in v8:
time: 132 us
  Pallas kernels  129 us (98%)
  local copies, waits for them, and re-layouts  2.07 us (2%)
    pallas_call x1, Pallas kernels, local_step(): pl.pallas_call(functools.partial(moe_kernel, n_ep, n_dp, capacity, src_ca...  129 us

profile of v8, /device:TPU:21, one launch (start us, length us, event | category | flops | bytes accessed | tf_op | source)
XLA Modules:
  0.0 131.7 jit_solution(5195135241054156332)
XLA Ops:
  0.0 0.0 copy-start
  0.0 0.0 copy-start.1
  0.0 128.8 %moe_layer.1 = (bf16[512,768]{1,0:T(8,128)(2,1)}, f32[1]{0:T(128)}) custom-call(bf16[512,768]{1,0:T(8,128)(2,1)} %x_ref.1, f32[64,512]{1,0:T(8,128)} %bitcast.28, bf16[4,768,3072]{2,1,0:T(8,128)(2,1)} %w1_hbm.1, bf16[4,3072,768]{2,1,0:T(8,128)(2,1)} %w2_hbm.1), custom_call_target="tpu_custom_call" | custom-call | tf_op jit(solution)/shard_map/moe_layer/pallas_call | solution.py:583
  129.6 0.0 copy-done
  129.6 0.0 copy-done.1
  129.6 2.1 %copy.24 = bf16[512,768]{1,0:T(8,128)(2,1)} copy(bf16[512,768]{1,0:T(8,128)(2,1)} %get-tuple-element.25) | data formatting | bytes 1572864
  (1 shorter events, 0.0 us)
Async XLA Ops:
  0.0 129.6 %copy-start = (f32[512,64]{0,1:T(8,128)S(1)}, f32[512,64]{0,1:T(8,128)}, u32[]{:S(2)}) copy-start(f32[512,64]{0,1:T(8,128)} %param.7) | copy-start | bytes 393220
  0.0 129.6 %copy-start.1 = (bf16[512,768]{1,0:T(8,128)(2,1)S(1)}, bf16[512,768]{1,0:T(8,128)(2,1)}, u32[]{:S(2)}) copy-start(bf16[512,768]{1,0:T(8,128)(2,1)} %x_ref.1) | copy-start | bytes 2359300
